TPU v7x, 32 devices: a 4x4x1 block of a 4x4x8 slice. The times are simulated.
32 devices in a mesh: member: 1 (over z), ty: 4 (over y), tx: 4 (over x), panel: 2 (over core).
Axes of the slice: x: 4, y: 4, z: 1, core: 2. Of those that a mesh axis runs over, the one named last changes fastest.
The devices are a block of a 4x4x8 slice.
Arguments:
- tracer: float32 [6, 1440, 1440], P(('member', 'panel'), 'tx', 'ty')
- wind_a: float32 [6, 1440, 1440], P('panel', 'tx', 'ty')
- wind_b: float32 [6, 1440, 1440], P('panel', 'tx', 'ty')
- wind_scale: float32 [16], replicated
Outputs:
- output: float32 [6, 1440, 1440], P(('member', 'panel'), 'tx', 'ty')
All inputs are finite; a program needn't handle non-finite values.
Results may differ from a plain program's by a relative error of at most 0.001.
Values sent between devices are 32-bit elements.
A program may use at most 768 MiB of HBM per device.

v0:
```python
import math
import jax
import jax.numpy as jnp
from jax import lax
from jax.sharding import PartitionSpec as P

C_SPEED = 2.5
CFL_STEP = 0.12
EDGE_TABLE = (
    ((3, 1, 0), (1, 0, 0), (5, 3, 0), (4, 2, 0)),
    ((0, 1, 0), (2, 0, 0), (5, 1, 1), (4, 1, 0)),
    ((1, 1, 0), (3, 0, 0), (5, 2, 1), (4, 3, 1)),
    ((2, 1, 0), (0, 0, 0), (5, 0, 0), (4, 0, 1)),
    ((3, 3, 1), (1, 3, 0), (0, 3, 0), (2, 3, 1)),
    ((3, 2, 0), (1, 2, 1), (2, 2, 1), (0, 2, 0)),
)


def edge_sign(side_id, edge_id):
    out_sign = 1.0 if edge_id in (1, 3) else -1.0
    return out_sign if side_id in (0, 2) else -out_sign


def out_strips(field_a, field_b):
    return (field_a[:, 0:2, :],
            jnp.flip(field_a[:, -2:, :], axis=1),
            jnp.swapaxes(field_b[:, :, 0:2], 1, 2),
            jnp.swapaxes(jnp.flip(field_b[:, :, -2:], axis=2), 1, 2))


def to_blocks(ghosts):
    return (jnp.flip(ghosts[0], axis=1), ghosts[1],
            jnp.swapaxes(jnp.flip(ghosts[2], axis=1), 1, 2), jnp.swapaxes(ghosts[3], 1, 2))


def extend_field(field_now, blocks):
    return (jnp.concatenate([blocks[0], field_now, blocks[1]], axis=1),
            jnp.concatenate([blocks[2], field_now, blocks[3]], axis=2))


def wind_faces(blocks, wind_a, wind_b):
    ext_a = jnp.concatenate([blocks[0][:, 1:2, :], wind_a, blocks[1][:, 0:1, :]], axis=1)
    ext_b = jnp.concatenate([blocks[2][:, :, 1:2], wind_b, blocks[3][:, :, 0:1]], axis=2)
    return 0.5 * (ext_a[:, :-1, :] + ext_a[:, 1:, :]), 0.5 * (ext_b[:, :, :-1] + ext_b[:, :, 1:])


def face_flux_div(ext_arr, wind_face, step_scale, axis_id):
    face_count = ext_arr.shape[axis_id] - 3
    far_left = lax.slice_in_dim(ext_arr, 0, face_count, axis=axis_id)
    near_left = lax.slice_in_dim(ext_arr, 1, face_count + 1, axis=axis_id)
    near_right = lax.slice_in_dim(ext_arr, 2, face_count + 2, axis=axis_id)
    far_right = lax.slice_in_dim(ext_arr, 3, face_count + 3, axis=axis_id)
    face_val = (7.0 * (near_left + near_right) - (far_left + far_right)) / 12.0
    face_flux = step_scale * wind_face * face_val - (0.5 * C_SPEED) * (near_right - near_left)
    return (lax.slice_in_dim(face_flux, 1, face_count, axis=axis_id)
            - lax.slice_in_dim(face_flux, 0, face_count - 1, axis=axis_id))


def tendency(ext_a, ext_b, face_a, face_b, step_scale, inv_area):
    div_total = face_flux_div(ext_a, face_a, step_scale, 1) + face_flux_div(ext_b, face_b, step_scale, 2)
    return -div_total * inv_area


def inverse_area(row_ids, col_ids, cells):
    dalpha = 0.5 * math.pi / cells
    tan_a = jnp.tan((row_ids.astype(jnp.float32) + 0.5) * dalpha - 0.25 * math.pi)[:, None]
    tan_b = jnp.tan((col_ids.astype(jnp.float32) + 0.5) * dalpha - 0.25 * math.pi)[None, :]
    r_sq = 1.0 + tan_a * tan_a + tan_b * tan_b
    sqrt_g = (1.0 + tan_a * tan_a) * (1.0 + tan_b * tan_b) / (r_sq * jnp.sqrt(r_sq))
    return 1.0 / (dalpha * sqrt_g)


def solution(mesh):
    tile_count = mesh.shape['tx']
    panel_count = mesh.shape['panel']
    local_panels = 6 // panel_count
    group_axes = ('ty', 'tx', 'panel')
    field_spec = P(('member', 'panel'), 'tx', 'ty')
    wind_spec = P('panel', 'tx', 'ty')
    shift_up = [(idx_src, idx_src + 1) for idx_src in range(tile_count - 1)]
    shift_down = [(idx_src + 1, idx_src) for idx_src in range(tile_count - 1)]

    def device_id(panel_dev, tile_pos):
        return (tile_pos[1] * tile_count + tile_pos[0]) * panel_count + panel_dev

    def edge_tile(side_id, along_idx):
        last_idx = tile_count - 1
        return ((0, along_idx), (last_idx, along_idx), (along_idx, 0), (along_idx, last_idx))[side_id]

    cross_plan = []
    for panel_id in range(6):
        for side_id in range(4):
            src_panel, edge_id, flipped = EDGE_TABLE[panel_id][side_id]
            perm_pairs = []
            for along_idx in range(tile_count):
                src_along = tile_count - 1 - along_idx if flipped else along_idx
                perm_pairs.append((device_id(src_panel // local_panels, edge_tile(edge_id, src_along)),
                                   device_id(panel_id // local_panels, edge_tile(side_id, along_idx))))
            cross_plan.append((panel_id % local_panels, side_id, src_panel % local_panels, edge_id, flipped, perm_pairs))

    def fill_halo(field_a, field_b, signed):
        strips = out_strips(field_a, field_b)
        received = {}
        for slot_id, side_id, src_slot, edge_id, flipped, perm_pairs in cross_plan:
            one_strip = strips[edge_id][src_slot]
            if flipped:
                one_strip = jnp.flip(one_strip, axis=1)
            if signed:
                one_strip = edge_sign(side_id, edge_id) * one_strip
            moved_strip = lax.ppermute(one_strip, group_axes, perm_pairs)
            received[(side_id, slot_id)] = received.get((side_id, slot_id), 0.0) + moved_strip
        cross_blks = to_blocks([jnp.stack([received[(side_id, slot_id)] for slot_id in range(local_panels)])
                                for side_id in range(4)])
        own_blks = (lax.ppermute(field_a[:, -2:, :], 'tx', shift_up),
                    lax.ppermute(field_a[:, 0:2, :], 'tx', shift_down),
                    lax.ppermute(field_b[:, :, -2:], 'ty', shift_up),
                    lax.ppermute(field_b[:, :, 0:2], 'ty', shift_down))
        return tuple(own_blk + cross_blk for own_blk, cross_blk in zip(own_blks, cross_blks))

    def local_run(tracer, wind_a, wind_b, wind_scale):
        tile_rows = tracer.shape[1]
        tile_cols = tracer.shape[2]
        cells = tile_rows * tile_count
        time_step = CFL_STEP * (0.5 * math.pi / cells)
        row_ids = lax.axis_index('tx') * tile_rows + jnp.arange(tile_rows)
        col_ids = lax.axis_index('ty') * tile_cols + jnp.arange(tile_cols)
        inv_area = inverse_area(row_ids, col_ids, cells)
        face_a, face_b = wind_faces(fill_halo(wind_a, wind_b, True), wind_a, wind_b)

        def tend_of(tracer_now, step_scale):
            ext_a, ext_b = extend_field(tracer_now, fill_halo(tracer_now, tracer_now, False))
            return tendency(ext_a, ext_b, face_a, face_b, step_scale, inv_area)

        def one_step(step_id, tracer_now):
            step_scale = wind_scale[step_id]
            stage_one = tracer_now + time_step * tend_of(tracer_now, step_scale)
            stage_two = stage_one + time_step * tend_of(stage_one, step_scale)
            return 0.5 * (tracer_now + stage_two)

        return lax.fori_loop(0, wind_scale.shape[0], one_step, tracer)

    return jax.shard_map(local_run, mesh=mesh, in_specs=(field_spec, wind_spec, wind_spec, P()),
                         out_specs=field_spec, check_vma=False)
```

profile of v0, /device:TPU:97, one launch (start us, length us, event | category | flops | bytes accessed | tf_op | source)
XLA Modules:
  0.0 2860.5 jit_solution(13007906161778518293)
XLA Ops:
  64.5 2794.8 %while.14 = (s32[]{:T(128)}, f32[3,360,360]{2,1,0:T(8,128)S(1)}, f32[16]{0:T(128)S(1)}, f32[3,361,360]{2,1,0:T(8,128)}, f32[3,360,361]{2,1,0:T(8,128)}, /*index=...) while((s32[]{:T(128)}, f32[3,360,360]{2,1,0:T(8,128)S(1)}, f32[16]{0:T(128)S(1)}, ...), condition=%wide.region_1.2_spmd.clone, body=%wide.region_0.1_spmd.clone.sunk | while | flops 28900800 | bytes 49896628 | solution.py:140
  83.9 12.2 collective-permute-start.15
  118.2 10.7 collective-permute-done.25
  162.2 10.9 collective-permute-start.43
  199.5 10.7 collective-permute-done.53
  255.9 12.2 collective-permute-start.15
  292.7 10.7 collective-permute-done.25
  336.6 10.9 collective-permute-start.43
  374.0 10.7 collective-permute-done.53
  430.4 12.2 collective-permute-start.15
  467.1 10.7 collective-permute-done.25
  511.1 10.9 collective-permute-start.43
  548.5 10.7 collective-permute-done.53
  604.8 12.2 collective-permute-start.15
  641.6 10.7 collective-permute-done.25
  685.6 10.9 collective-permute-start.43
  722.9 10.7 collective-permute-done.53
  779.3 12.2 collective-permute-start.15
  816.1 10.7 collective-permute-done.25
  860.0 10.9 collective-permute-start.43
  897.4 10.7 collective-permute-done.53
  953.8 12.2 collective-permute-start.15
  990.5 10.7 collective-permute-done.25
  1034.5 10.9 collective-permute-start.43
  1071.9 10.7 collective-permute-done.53
  1128.2 12.2 collective-permute-start.15
  1209.0 10.9 collective-permute-start.43
  1302.7 12.2 collective-permute-start.15
  1383.4 10.9 collective-permute-start.43
  1420.8 10.7 collective-permute-done.53
  1477.2 12.2 collective-permute-start.15
  1513.9 10.7 collective-permute-done.25
  1557.9 10.9 collective-permute-start.43
  1651.6 12.2 collective-permute-start.15
  1732.4 10.9 collective-permute-start.43
  1826.1 12.2 collective-permute-start.15
  1862.9 10.7 collective-permute-done.25
  1906.8 10.9 collective-permute-start.43
  2000.6 12.2 collective-permute-start.15
  2081.3 10.9 collective-permute-start.43
  2175.0 12.2 collective-permute-start.15
  2255.8 10.9 collective-permute-start.43
  2349.5 12.2 collective-permute-start.15
  2430.2 10.9 collective-permute-start.43
  2524.0 12.2 collective-permute-start.15
  2604.7 10.9 collective-permute-start.43
  2698.4 12.2 collective-permute-start.15
  2779.2 10.9 collective-permute-start.43
  (3627 shorter events, 2309.1 us)
Async XLA Ops:
  65.3 52.2 %collective-permute-start.24 = (f32[2,360]{1,0:T(2,128)S(1)}, f32[2,360]{1,0:T(2,128)S(1)}, u32[]{:S(2)}, u32[]{:S(2)}) collective-permute-start(f32[2,360]{1,0:T(2,128)S(1)} %bitcast.318), channel_id=1, source_target_pairs={{6,0},{14,8},{22,16},{30,24}} | collective-permute-start | bytes 8648 | tf_op jit(solution)/shard_map/while/body/eval_jaxpr/ppermute | solution.py:110
  66.8 48.7 %collective-permute-start.3 = (f32[2,360]{1,0:T(2,128)S(1)}, f32[2,360]{1,0:T(2,128)S(1)}, u32[]{:S(2)}, u32[]{:S(2)}) collective-permute-start(f32[2,360]{1,0:T(2,128)S(1)} %bitcast.322), channel_id=1, source_target_pairs={{7,24},{15,26},{23,28},{31,30}} | collective-permute-start | bytes 8648 | tf_op jit(solution)/shard_map/while/body/eval_jaxpr/ppermute | solution.py:110
  151.0 47.9 %collective-permute-start.52 = (f32[2,360]{1,0:T(2,128)S(1)}, f32[2,360]{1,0:T(2,128)S(1)}, u32[]{:S(2)}, u32[]{:S(2)}) collective-permute-start(f32[2,360]{1,0:T(2,128)S(1)} %bitcast.320), channel_id=1, source_target_pairs={{6,0},{14,8},{22,16},{30,24}} | collective-permute-start | bytes 8648 | tf_op jit(solution)/shard_map/while/body/eval_jaxpr/ppermute | solution.py:110
  243.1 48.9 %collective-permute-start.24 = (f32[2,360]{1,0:T(2,128)S(1)}, f32[2,360]{1,0:T(2,128)S(1)}, u32[]{:S(2)}, u32[]{:S(2)}) collective-permute-start(f32[2,360]{1,0:T(2,128)S(1)} %bitcast.318), channel_id=1, source_target_pairs={{6,0},{14,8},{22,16},{30,24}} | collective-permute-start | bytes 8648 | tf_op jit(solution)/shard_map/while/body/eval_jaxpr/ppermute | solution.py:110
  244.6 45.4 %collective-permute-start.3 = (f32[2,360]{1,0:T(2,128)S(1)}, f32[2,360]{1,0:T(2,128)S(1)}, u32[]{:S(2)}, u32[]{:S(2)}) collective-permute-start(f32[2,360]{1,0:T(2,128)S(1)} %bitcast.322), channel_id=1, source_target_pairs={{7,24},{15,26},{23,28},{31,30}} | collective-permute-start | bytes 8648 | tf_op jit(solution)/shard_map/while/body/eval_jaxpr/ppermute | solution.py:110
  325.4 47.9 %collective-permute-start.52 = (f32[2,360]{1,0:T(2,128)S(1)}, f32[2,360]{1,0:T(2,128)S(1)}, u32[]{:S(2)}, u32[]{:S(2)}) collective-permute-start(f32[2,360]{1,0:T(2,128)S(1)} %bitcast.320), channel_id=1, source_target_pairs={{6,0},{14,8},{22,16},{30,24}} | collective-permute-start | bytes 8648 | tf_op jit(solution)/shard_map/while/body/eval_jaxpr/ppermute | solution.py:110
  417.6 48.9 %collective-permute-start.24 = (f32[2,360]{1,0:T(2,128)S(1)}, f32[2,360]{1,0:T(2,128)S(1)}, u32[]{:S(2)}, u32[]{:S(2)}) collective-permute-start(f32[2,360]{1,0:T(2,128)S(1)} %bitcast.318), channel_id=1, source_target_pairs={{6,0},{14,8},{22,16},{30,24}} | collective-permute-start | bytes 8648 | tf_op jit(solution)/shard_map/while/body/eval_jaxpr/ppermute | solution.py:110
  419.0 45.4 %collective-permute-start.3 = (f32[2,360]{1,0:T(2,128)S(1)}, f32[2,360]{1,0:T(2,128)S(1)}, u32[]{:S(2)}, u32[]{:S(2)}) collective-permute-start(f32[2,360]{1,0:T(2,128)S(1)} %bitcast.322), channel_id=1, source_target_pairs={{7,24},{15,26},{23,28},{31,30}} | collective-permute-start | bytes 8648 | tf_op jit(solution)/shard_map/while/body/eval_jaxpr/ppermute | solution.py:110
  499.9 47.9 %collective-permute-start.52 = (f32[2,360]{1,0:T(2,128)S(1)}, f32[2,360]{1,0:T(2,128)S(1)}, u32[]{:S(2)}, u32[]{:S(2)}) collective-permute-start(f32[2,360]{1,0:T(2,128)S(1)} %bitcast.320), channel_id=1, source_target_pairs={{6,0},{14,8},{22,16},{30,24}} | collective-permute-start | bytes 8648 | tf_op jit(solution)/shard_map/while/body/eval_jaxpr/ppermute | solution.py:110
  592.1 48.9 %collective-permute-start.24 = (f32[2,360]{1,0:T(2,128)S(1)}, f32[2,360]{1,0:T(2,128)S(1)}, u32[]{:S(2)}, u32[]{:S(2)}) collective-permute-start(f32[2,360]{1,0:T(2,128)S(1)} %bitcast.318), channel_id=1, source_target_pairs={{6,0},{14,8},{22,16},{30,24}} | collective-permute-start | bytes 8648 | tf_op jit(solution)/shard_map/while/body/eval_jaxpr/ppermute | solution.py:110
  593.5 45.4 %collective-permute-start.3 = (f32[2,360]{1,0:T(2,128)S(1)}, f32[2,360]{1,0:T(2,128)S(1)}, u32[]{:S(2)}, u32[]{:S(2)}) collective-permute-start(f32[2,360]{1,0:T(2,128)S(1)} %bitcast.322), channel_id=1, source_target_pairs={{7,24},{15,26},{23,28},{31,30}} | collective-permute-start | bytes 8648 | tf_op jit(solution)/shard_map/while/body/eval_jaxpr/ppermute | solution.py:110
  674.4 47.9 %collective-permute-start.52 = (f32[2,360]{1,0:T(2,128)S(1)}, f32[2,360]{1,0:T(2,128)S(1)}, u32[]{:S(2)}, u32[]{:S(2)}) collective-permute-start(f32[2,360]{1,0:T(2,128)S(1)} %bitcast.320), channel_id=1, source_target_pairs={{6,0},{14,8},{22,16},{30,24}} | collective-permute-start | bytes 8648 | tf_op jit(solution)/shard_map/while/body/eval_jaxpr/ppermute | solution.py:110
  766.5 48.9 %collective-permute-start.24 = (f32[2,360]{1,0:T(2,128)S(1)}, f32[2,360]{1,0:T(2,128)S(1)}, u32[]{:S(2)}, u32[]{:S(2)}) collective-permute-start(f32[2,360]{1,0:T(2,128)S(1)} %bitcast.318), channel_id=1, source_target_pairs={{6,0},{14,8},{22,16},{30,24}} | collective-permute-start | bytes 8648 | tf_op jit(solution)/shard_map/while/body/eval_jaxpr/ppermute | solution.py:110
  768.0 45.4 %collective-permute-start.3 = (f32[2,360]{1,0:T(2,128)S(1)}, f32[2,360]{1,0:T(2,128)S(1)}, u32[]{:S(2)}, u32[]{:S(2)}) collective-permute-start(f32[2,360]{1,0:T(2,128)S(1)} %bitcast.322), channel_id=1, source_target_pairs={{7,24},{15,26},{23,28},{31,30}} | collective-permute-start | bytes 8648 | tf_op jit(solution)/shard_map/while/body/eval_jaxpr/ppermute | solution.py:110
  848.8 47.9 %collective-permute-start.52 = (f32[2,360]{1,0:T(2,128)S(1)}, f32[2,360]{1,0:T(2,128)S(1)}, u32[]{:S(2)}, u32[]{:S(2)}) collective-permute-start(f32[2,360]{1,0:T(2,128)S(1)} %bitcast.320), channel_id=1, source_target_pairs={{6,0},{14,8},{22,16},{30,24}} | collective-permute-start | bytes 8648 | tf_op jit(solution)/shard_map/while/body/eval_jaxpr/ppermute | solution.py:110
  941.0 48.9 %collective-permute-start.24 = (f32[2,360]{1,0:T(2,128)S(1)}, f32[2,360]{1,0:T(2,128)S(1)}, u32[]{:S(2)}, u32[]{:S(2)}) collective-permute-start(f32[2,360]{1,0:T(2,128)S(1)} %bitcast.318), channel_id=1, source_target_pairs={{6,0},{14,8},{22,16},{30,24}} | collective-permute-start | bytes 8648 | tf_op jit(solution)/shard_map/while/body/eval_jaxpr/ppermute | solution.py:110
  942.4 45.4 %collective-permute-start.3 = (f32[2,360]{1,0:T(2,128)S(1)}, f32[2,360]{1,0:T(2,128)S(1)}, u32[]{:S(2)}, u32[]{:S(2)}) collective-permute-start(f32[2,360]{1,0:T(2,128)S(1)} %bitcast.322), channel_id=1, source_target_pairs={{7,24},{15,26},{23,28},{31,30}} | collective-permute-start | bytes 8648 | tf_op jit(solution)/shard_map/while/body/eval_jaxpr/ppermute | solution.py:110
  1023.3 47.9 %collective-permute-start.52 = (f32[2,360]{1,0:T(2,128)S(1)}, f32[2,360]{1,0:T(2,128)S(1)}, u32[]{:S(2)}, u32[]{:S(2)}) collective-permute-start(f32[2,360]{1,0:T(2,128)S(1)} %bitcast.320), channel_id=1, source_target_pairs={{6,0},{14,8},{22,16},{30,24}} | collective-permute-start | bytes 8648 | tf_op jit(solution)/shard_map/while/body/eval_jaxpr/ppermute | solution.py:110
  1115.5 48.9 %collective-permute-start.24 = (f32[2,360]{1,0:T(2,128)S(1)}, f32[2,360]{1,0:T(2,128)S(1)}, u32[]{:S(2)}, u32[]{:S(2)}) collective-permute-start(f32[2,360]{1,0:T(2,128)S(1)} %bitcast.318), channel_id=1, source_target_pairs={{6,0},{14,8},{22,16},{30,24}} | collective-permute-start | bytes 8648 | tf_op jit(solution)/shard_map/while/body/eval_jaxpr/ppermute | solution.py:110
  1116.9 45.4 %collective-permute-start.3 = (f32[2,360]{1,0:T(2,128)S(1)}, f32[2,360]{1,0:T(2,128)S(1)}, u32[]{:S(2)}, u32[]{:S(2)}) collective-permute-start(f32[2,360]{1,0:T(2,128)S(1)} %bitcast.322), channel_id=1, source_target_pairs={{7,24},{15,26},{23,28},{31,30}} | collective-permute-start | bytes 8648 | tf_op jit(solution)/shard_map/while/body/eval_jaxpr/ppermute | solution.py:110
  1197.8 47.9 %collective-permute-start.52 = (f32[2,360]{1,0:T(2,128)S(1)}, f32[2,360]{1,0:T(2,128)S(1)}, u32[]{:S(2)}, u32[]{:S(2)}) collective-permute-start(f32[2,360]{1,0:T(2,128)S(1)} %bitcast.320), channel_id=1, source_target_pairs={{6,0},{14,8},{22,16},{30,24}} | collective-permute-start | bytes 8648 | tf_op jit(solution)/shard_map/while/body/eval_jaxpr/ppermute | solution.py:110
  1289.9 48.9 %collective-permute-start.24 = (f32[2,360]{1,0:T(2,128)S(1)}, f32[2,360]{1,0:T(2,128)S(1)}, u32[]{:S(2)}, u32[]{:S(2)}) collective-permute-start(f32[2,360]{1,0:T(2,128)S(1)} %bitcast.318), channel_id=1, source_target_pairs={{6,0},{14,8},{22,16},{30,24}} | collective-permute-start | bytes 8648 | tf_op jit(solution)/shard_map/while/body/eval_jaxpr/ppermute | solution.py:110
  1291.4 45.4 %collective-permute-start.3 = (f32[2,360]{1,0:T(2,128)S(1)}, f32[2,360]{1,0:T(2,128)S(1)}, u32[]{:S(2)}, u32[]{:S(2)}) collective-permute-start(f32[2,360]{1,0:T(2,128)S(1)} %bitcast.322), channel_id=1, source_target_pairs={{7,24},{15,26},{23,28},{31,30}} | collective-permute-start | bytes 8648 | tf_op jit(solution)/shard_map/while/body/eval_jaxpr/ppermute | solution.py:110
  1372.2 47.9 %collective-permute-start.52 = (f32[2,360]{1,0:T(2,128)S(1)}, f32[2,360]{1,0:T(2,128)S(1)}, u32[]{:S(2)}, u32[]{:S(2)}) collective-permute-start(f32[2,360]{1,0:T(2,128)S(1)} %bitcast.320), channel_id=1, source_target_pairs={{6,0},{14,8},{22,16},{30,24}} | collective-permute-start | bytes 8648 | tf_op jit(solution)/shard_map/while/body/eval_jaxpr/ppermute | solution.py:110
  1464.4 48.9 %collective-permute-start.24 = (f32[2,360]{1,0:T(2,128)S(1)}, f32[2,360]{1,0:T(2,128)S(1)}, u32[]{:S(2)}, u32[]{:S(2)}) collective-permute-start(f32[2,360]{1,0:T(2,128)S(1)} %bitcast.318), channel_id=1, source_target_pairs={{6,0},{14,8},{22,16},{30,24}} | collective-permute-start | bytes 8648 | tf_op jit(solution)/shard_map/while/body/eval_jaxpr/ppermute | solution.py:110
  1465.8 45.4 %collective-permute-start.3 = (f32[2,360]{1,0:T(2,128)S(1)}, f32[2,360]{1,0:T(2,128)S(1)}, u32[]{:S(2)}, u32[]{:S(2)}) collective-permute-start(f32[2,360]{1,0:T(2,128)S(1)} %bitcast.322), channel_id=1, source_target_pairs={{7,24},{15,26},{23,28},{31,30}} | collective-permute-start | bytes 8648 | tf_op jit(solution)/shard_map/while/body/eval_jaxpr/ppermute | solution.py:110
  1546.7 47.9 %collective-permute-start.52 = (f32[2,360]{1,0:T(2,128)S(1)}, f32[2,360]{1,0:T(2,128)S(1)}, u32[]{:S(2)}, u32[]{:S(2)}) collective-permute-start(f32[2,360]{1,0:T(2,128)S(1)} %bitcast.320), channel_id=1, source_target_pairs={{6,0},{14,8},{22,16},{30,24}} | collective-permute-start | bytes 8648 | tf_op jit(solution)/shard_map/while/body/eval_jaxpr/ppermute | solution.py:110
  1638.8 48.9 %collective-permute-start.24 = (f32[2,360]{1,0:T(2,128)S(1)}, f32[2,360]{1,0:T(2,128)S(1)}, u32[]{:S(2)}, u32[]{:S(2)}) collective-permute-start(f32[2,360]{1,0:T(2,128)S(1)} %bitcast.318), channel_id=1, source_target_pairs={{6,0},{14,8},{22,16},{30,24}} | collective-permute-start | bytes 8648 | tf_op jit(solution)/shard_map/while/body/eval_jaxpr/ppermute | solution.py:110
  1640.3 45.4 %collective-permute-start.3 = (f32[2,360]{1,0:T(2,128)S(1)}, f32[2,360]{1,0:T(2,128)S(1)}, u32[]{:S(2)}, u32[]{:S(2)}) collective-permute-start(f32[2,360]{1,0:T(2,128)S(1)} %bitcast.322), channel_id=1, source_target_pairs={{7,24},{15,26},{23,28},{31,30}} | collective-permute-start | bytes 8648 | tf_op jit(solution)/shard_map/while/body/eval_jaxpr/ppermute | solution.py:110
  1721.2 47.9 %collective-permute-start.52 = (f32[2,360]{1,0:T(2,128)S(1)}, f32[2,360]{1,0:T(2,128)S(1)}, u32[]{:S(2)}, u32[]{:S(2)}) collective-permute-start(f32[2,360]{1,0:T(2,128)S(1)} %bitcast.320), channel_id=1, source_target_pairs={{6,0},{14,8},{22,16},{30,24}} | collective-permute-start | bytes 8648 | tf_op jit(solution)/shard_map/while/body/eval_jaxpr/ppermute | solution.py:110
  1813.3 48.9 %collective-permute-start.24 = (f32[2,360]{1,0:T(2,128)S(1)}, f32[2,360]{1,0:T(2,128)S(1)}, u32[]{:S(2)}, u32[]{:S(2)}) collective-permute-start(f32[2,360]{1,0:T(2,128)S(1)} %bitcast.318), channel_id=1, source_target_pairs={{6,0},{14,8},{22,16},{30,24}} | collective-permute-start | bytes 8648 | tf_op jit(solution)/shard_map/while/body/eval_jaxpr/ppermute | solution.py:110
  1814.8 45.4 %collective-permute-start.3 = (f32[2,360]{1,0:T(2,128)S(1)}, f32[2,360]{1,0:T(2,128)S(1)}, u32[]{:S(2)}, u32[]{:S(2)}) collective-permute-start(f32[2,360]{1,0:T(2,128)S(1)} %bitcast.322), channel_id=1, source_target_pairs={{7,24},{15,26},{23,28},{31,30}} | collective-permute-start | bytes 8648 | tf_op jit(solution)/shard_map/while/body/eval_jaxpr/ppermute | solution.py:110
  1895.6 47.9 %collective-permute-start.52 = (f32[2,360]{1,0:T(2,128)S(1)}, f32[2,360]{1,0:T(2,128)S(1)}, u32[]{:S(2)}, u32[]{:S(2)}) collective-permute-start(f32[2,360]{1,0:T(2,128)S(1)} %bitcast.320), channel_id=1, source_target_pairs={{6,0},{14,8},{22,16},{30,24}} | collective-permute-start | bytes 8648 | tf_op jit(solution)/shard_map/while/body/eval_jaxpr/ppermute | solution.py:110
  1987.8 48.9 %collective-permute-start.24 = (f32[2,360]{1,0:T(2,128)S(1)}, f32[2,360]{1,0:T(2,128)S(1)}, u32[]{:S(2)}, u32[]{:S(2)}) collective-permute-start(f32[2,360]{1,0:T(2,128)S(1)} %bitcast.318), channel_id=1, source_target_pairs={{6,0},{14,8},{22,16},{30,24}} | collective-permute-start | bytes 8648 | tf_op jit(solution)/shard_map/while/body/eval_jaxpr/ppermute | solution.py:110
  1989.2 45.4 %collective-permute-start.3 = (f32[2,360]{1,0:T(2,128)S(1)}, f32[2,360]{1,0:T(2,128)S(1)}, u32[]{:S(2)}, u32[]{:S(2)}) collective-permute-start(f32[2,360]{1,0:T(2,128)S(1)} %bitcast.322), channel_id=1, source_target_pairs={{7,24},{15,26},{23,28},{31,30}} | collective-permute-start | bytes 8648 | tf_op jit(solution)/shard_map/while/body/eval_jaxpr/ppermute | solution.py:110
  2070.1 47.9 %collective-permute-start.52 = (f32[2,360]{1,0:T(2,128)S(1)}, f32[2,360]{1,0:T(2,128)S(1)}, u32[]{:S(2)}, u32[]{:S(2)}) collective-permute-start(f32[2,360]{1,0:T(2,128)S(1)} %bitcast.320), channel_id=1, source_target_pairs={{6,0},{14,8},{22,16},{30,24}} | collective-permute-start | bytes 8648 | tf_op jit(solution)/shard_map/while/body/eval_jaxpr/ppermute | solution.py:110
  2162.2 48.9 %collective-permute-start.24 = (f32[2,360]{1,0:T(2,128)S(1)}, f32[2,360]{1,0:T(2,128)S(1)}, u32[]{:S(2)}, u32[]{:S(2)}) collective-permute-start(f32[2,360]{1,0:T(2,128)S(1)} %bitcast.318), channel_id=1, source_target_pairs={{6,0},{14,8},{22,16},{30,24}} | collective-permute-start | bytes 8648 | tf_op jit(solution)/shard_map/while/body/eval_jaxpr/ppermute | solution.py:110
  2163.7 45.4 %collective-permute-start.3 = (f32[2,360]{1,0:T(2,128)S(1)}, f32[2,360]{1,0:T(2,128)S(1)}, u32[]{:S(2)}, u32[]{:S(2)}) collective-permute-start(f32[2,360]{1,0:T(2,128)S(1)} %bitcast.322), channel_id=1, source_target_pairs={{7,24},{15,26},{23,28},{31,30}} | collective-permute-start | bytes 8648 | tf_op jit(solution)/shard_map/while/body/eval_jaxpr/ppermute | solution.py:110
  2244.6 47.9 %collective-permute-start.52 = (f32[2,360]{1,0:T(2,128)S(1)}, f32[2,360]{1,0:T(2,128)S(1)}, u32[]{:S(2)}, u32[]{:S(2)}) collective-permute-start(f32[2,360]{1,0:T(2,128)S(1)} %bitcast.320), channel_id=1, source_target_pairs={{6,0},{14,8},{22,16},{30,24}} | collective-permute-start | bytes 8648 | tf_op jit(solution)/shard_map/while/body/eval_jaxpr/ppermute | solution.py:110
  2336.7 48.9 %collective-permute-start.24 = (f32[2,360]{1,0:T(2,128)S(1)}, f32[2,360]{1,0:T(2,128)S(1)}, u32[]{:S(2)}, u32[]{:S(2)}) collective-permute-start(f32[2,360]{1,0:T(2,128)S(1)} %bitcast.318), channel_id=1, source_target_pairs={{6,0},{14,8},{22,16},{30,24}} | collective-permute-start | bytes 8648 | tf_op jit(solution)/shard_map/while/body/eval_jaxpr/ppermute | solution.py:110
  2338.2 45.4 %collective-permute-start.3 = (f32[2,360]{1,0:T(2,128)S(1)}, f32[2,360]{1,0:T(2,128)S(1)}, u32[]{:S(2)}, u32[]{:S(2)}) collective-permute-start(f32[2,360]{1,0:T(2,128)S(1)} %bitcast.322), channel_id=1, source_target_pairs={{7,24},{15,26},{23,28},{31,30}} | collective-permute-start | bytes 8648 | tf_op jit(solution)/shard_map/while/body/eval_jaxpr/ppermute | solution.py:110
  2419.0 47.9 %collective-permute-start.52 = (f32[2,360]{1,0:T(2,128)S(1)}, f32[2,360]{1,0:T(2,128)S(1)}, u32[]{:S(2)}, u32[]{:S(2)}) collective-permute-start(f32[2,360]{1,0:T(2,128)S(1)} %bitcast.320), channel_id=1, source_target_pairs={{6,0},{14,8},{22,16},{30,24}} | collective-permute-start | bytes 8648 | tf_op jit(solution)/shard_map/while/body/eval_jaxpr/ppermute | solution.py:110
  2511.2 48.9 %collective-permute-start.24 = (f32[2,360]{1,0:T(2,128)S(1)}, f32[2,360]{1,0:T(2,128)S(1)}, u32[]{:S(2)}, u32[]{:S(2)}) collective-permute-start(f32[2,360]{1,0:T(2,128)S(1)} %bitcast.318), channel_id=1, source_target_pairs={{6,0},{14,8},{22,16},{30,24}} | collective-permute-start | bytes 8648 | tf_op jit(solution)/shard_map/while/body/eval_jaxpr/ppermute | solution.py:110
  2512.6 45.4 %collective-permute-start.3 = (f32[2,360]{1,0:T(2,128)S(1)}, f32[2,360]{1,0:T(2,128)S(1)}, u32[]{:S(2)}, u32[]{:S(2)}) collective-permute-start(f32[2,360]{1,0:T(2,128)S(1)} %bitcast.322), channel_id=1, source_target_pairs={{7,24},{15,26},{23,28},{31,30}} | collective-permute-start | bytes 8648 | tf_op jit(solution)/shard_map/while/body/eval_jaxpr/ppermute | solution.py:110
  2593.5 47.9 %collective-permute-start.52 = (f32[2,360]{1,0:T(2,128)S(1)}, f32[2,360]{1,0:T(2,128)S(1)}, u32[]{:S(2)}, u32[]{:S(2)}) collective-permute-start(f32[2,360]{1,0:T(2,128)S(1)} %bitcast.320), channel_id=1, source_target_pairs={{6,0},{14,8},{22,16},{30,24}} | collective-permute-start | bytes 8648 | tf_op jit(solution)/shard_map/while/body/eval_jaxpr/ppermute | solution.py:110
  2685.6 48.9 %collective-permute-start.24 = (f32[2,360]{1,0:T(2,128)S(1)}, f32[2,360]{1,0:T(2,128)S(1)}, u32[]{:S(2)}, u32[]{:S(2)}) collective-permute-start(f32[2,360]{1,0:T(2,128)S(1)} %bitcast.318), channel_id=1, source_target_pairs={{6,0},{14,8},{22,16},{30,24}} | collective-permute-start | bytes 8648 | tf_op jit(solution)/shard_map/while/body/eval_jaxpr/ppermute | solution.py:110
  2687.1 45.4 %collective-permute-start.3 = (f32[2,360]{1,0:T(2,128)S(1)}, f32[2,360]{1,0:T(2,128)S(1)}, u32[]{:S(2)}, u32[]{:S(2)}) collective-permute-start(f32[2,360]{1,0:T(2,128)S(1)} %bitcast.322), channel_id=1, source_target_pairs={{7,24},{15,26},{23,28},{31,30}} | collective-permute-start | bytes 8648 | tf_op jit(solution)/shard_map/while/body/eval_jaxpr/ppermute | solution.py:110
  2768.0 47.9 %collective-permute-start.52 = (f32[2,360]{1,0:T(2,128)S(1)}, f32[2,360]{1,0:T(2,128)S(1)}, u32[]{:S(2)}, u32[]{:S(2)}) collective-permute-start(f32[2,360]{1,0:T(2,128)S(1)} %bitcast.320), channel_id=1, source_target_pairs={{6,0},{14,8},{22,16},{30,24}} | collective-permute-start | bytes 8648 | tf_op jit(solution)/shard_map/while/body/eval_jaxpr/ppermute | solution.py:110
  (929 other events, 10335.6 us)
where the time goes:
time: 2890 us; the launch traced here: 2860 us
  starting transfers between devices  1680 us (58%)
  waiting for transfers between devices  460 us (16%)
  local copies, waits for them, and re-layouts  358 us (12%)
  other arithmetic  339 us (12%)
    ppermute x792, starting transfers between devices, fill_halo(): moved_strip = lax.ppermute(one_strip, group_axes, perm_pairs)  1420 us
    ppermute x792, waiting for transfers between devices, fill_halo(): moved_strip = lax.ppermute(one_strip, group_axes, perm_pairs)  419 us
    sub x64, other arithmetic, face_flux_div(): step_scale * wind_face * face_val - 0.5 * C_SPEED * (near_right - near_left)  225 us
    while x592, local copies, waits for them, and re-layouts  136 us
    ppermute x33, starting transfers between devices, fill_halo(): lax.ppermute(field_a[:, -2:, :], 'tx', shift_up)  134 us
    rev x33, local copies, waits for them, and re-layouts, to_blocks(): jnp.flip(ghosts[2], axis=1)  91.5 us
  transfers between devices with their start and end apart: 924, of which 97 were waited for; matrix products, arithmetic and copies ran while one was open for 19% of the time, Pallas kernels for 0%

commit v1 on v0

v1 whole, which is shorter than its diff:
```python
import math
import jax
import jax.numpy as jnp
from jax import lax
from jax.experimental import pallas as pl
from jax.experimental.pallas import tpu as pltpu
from jax.sharding import PartitionSpec as P

C_SPEED = 2.5
CFL_STEP = 0.12
EDGE_CODE = (
    (310, 100, 530, 420), (10, 200, 511, 410), (110, 300, 521, 431),
    (210, 0, 500, 401), (331, 130, 30, 231), (320, 121, 221, 20),
)
H = 12
KR = 48
NPAN = 3
NC = 3
SB = 8
LN = 128
GL = 4
STEPS_PER_BLOCK = 3
BETA_ROWS = 4
F32 = jnp.float32
PLANES = range(NC)
SIDES = range(4)


def turned_sign(side_id, edge_id):
    return int(side_id % 2 == edge_id % 2)


def small_tan(v):
    sq = v * v
    sin_sum, cos_sum = jnp.full_like(v, 1.0), jnp.full_like(v, 1.0)
    for n in (6, 5, 4, 3, 2, 1):
        sin_sum = 1.0 - sq * sin_sum * (1.0 / (2 * n * (2 * n + 1)))
        cos_sum = 1.0 - sq * cos_sum * (1.0 / (2 * n * (2 * n - 1)))
    return v * sin_sum / cos_sum


def lanes_of(shape):
    return lax.broadcasted_iota(jnp.int32, shape, len(shape) - 1)


def rows_of(shape):
    return lax.broadcasted_iota(jnp.int32, shape, len(shape) - 2)


def make_kernel(tile_count, steps, n_blocks, tile_rows):
    last = tile_count - 1
    cells = tile_rows * tile_count
    dalpha = 0.5 * math.pi / cells

    def kernel(ws_ref, q_in, a_in, b_in, out_ref, QA, QB, WW, CQ, KK, NN, TT, ZS, SEND, RECV, CSEND, CRECV,
               send_sem, recv_sem, csend_sem, crecv_sem):
        dev = lax.axis_index('panel')
        tx = lax.axis_index('tx')
        ty = lax.axis_index('ty')
        WA, WB = 0, NPAN

        def at_edge(side):
            return (tx == 0, tx == last, ty == 0, ty == last)[side]

        def edge_codes(p):
            g = NPAN * dev + p
            out = []
            for side in SIDES:
                codes = [row[side] * 2 + turned_sign(side, row[side] // 10 % 10) for row in EDGE_CODE]
                code = jnp.int32(codes[0])
                for n in range(1, len(codes)):
                    code = jnp.where(g == n, codes[n], code)
                turned, code = lax.rem(code, 2), lax.div(code, 2)
                panel = lax.div(code, 100)
                rest = code - 100 * panel
                dside = lax.div(rest, 10)
                flip = rest - 10 * dside
                out.append((lax.div(panel, NPAN), lax.rem(panel, NPAN), dside, jnp.where(at_edge(side), flip, 0),
                            jnp.where(at_edge(side), turned, 0), flip))
            return out

        def dest(codes, p, side, off):
            along = (ty if side < 2 else tx) + off
            edge = at_edge(side)
            d_dev, d_slot, dside, flip_here, _, flip = codes[side]
            al = along + flip * (last - 2 * along)
            c_tx = jnp.where(dside == 0, 0, jnp.where(dside == 1, last, al))
            c_ty = jnp.where(dside == 2, 0, jnp.where(dside == 3, last, al))
            step = 2 * (side % 2) - 1
            in_tx, in_ty = (tx + step, ty + off) if side < 2 else (tx + off, ty + step)
            device = {'tx': jnp.where(edge, c_tx, in_tx), 'ty': jnp.where(edge, c_ty, in_ty),
                      'panel': jnp.where(edge, d_dev, dev)}
            return device, jnp.where(edge, d_slot, p), jnp.where(edge, dside, side ^ 1), flip_here

        def corner_plan(codes, p, sa, sb):
            out_b = at_edge(2 + sb)
            plans = []
            for side, end, off in ((sa, sb, 2 * sb - 1), (2 + sb, sa, 2 * sa - 1)):
                device, slot, dside, flip = dest(codes, p, side, off)
                x = end + flip * (1 - 2 * end)
                e = 1 - x
                plans.append((device, slot, jnp.where(dside < 2, 2 * dside + e, 2 * e + (dside - 2)), side, x))
            (dv_a, sl_a, dc_a, s_a, x_a), (dv_b, sl_b, dc_b, s_b, x_b) = plans
            device = {key: jnp.where(out_b, dv_b[key], dv_a[key]) for key in dv_a}
            return (device, jnp.where(out_b, sl_b, sl_a), jnp.where(out_b, dc_b, dc_a),
                    jnp.where(out_b, s_b, s_a), jnp.where(out_b, x_b, x_a))

        def has_corner(sa, sb):
            return jnp.logical_not(jnp.logical_and(at_edge(sa), at_edge(2 + sb)))

        def is_here(device):
            return jnp.logical_and(jnp.logical_and(device['tx'] == tx, device['ty'] == ty), device['panel'] == dev)

        corners = [(sa, sb) for sa in range(2) for sb in range(2)]
        mesh_ids = pl.DeviceIdType.MESH

        barrier = pltpu.get_barrier_semaphore()

        @pl.loop(0, NPAN)
        def _(p):
            codes = edge_codes(p)
            for side in SIDES:
                pl.semaphore_signal(barrier, inc=1, device_id=dest(codes, p, side, 0)[0], device_id_type=mesh_ids)
            for sa, sb in corners:
                @pl.when(has_corner(sa, sb))
                def _():
                    pl.semaphore_signal(barrier, inc=1, device_id=corner_plan(codes, p, sa, sb)[0], device_id_type=mesh_ids)

        def load_field(in_ref, dst, base):
            @pl.loop(0, NPAN)
            def _(p):
                for it in PLANES:
                    for jt in PLANES:
                        TT[it, pl.ds(H + LN * jt, LN), :] = in_ref[p, pl.ds(LN * it, LN), pl.ds(LN * jt, LN)].T
                    for c in PLANES:
                        NN[c, pl.ds(H + LN * it, LN), :] = TT[it, pl.ds(c, LN, stride=NC), :].T

                @pl.loop(0, KR // SB)
                def _(kb):
                    for c in PLANES:
                        for k in range(SB):
                            dst[base + p, c, pl.ds(pl.multiple_of(64 * kb + SB * (k + 2), SB), SB), :] = NN[c, pl.ds(SB * kb + k, SB, stride=KR), :]

        def store_field(src):
            @pl.loop(0, NPAN)
            def _(p):
                @pl.loop(0, KR // SB)
                def _(kb):
                    for c in PLANES:
                        for k in range(SB):
                            NN[c, pl.ds(SB * kb + k, SB, stride=KR), :] = src[p, c, pl.ds(pl.multiple_of(64 * kb + SB * (k + 2), SB), SB), :]
                for it in PLANES:
                    for c in PLANES:
                        TT[it, pl.ds(c, LN, stride=NC), :] = NN[c, pl.ds(H + LN * it, LN), :].T
                    for jt in PLANES:
                        out_ref[p, pl.ds(LN * it, LN), pl.ds(LN * jt, LN)] = TT[it, pl.ds(H + LN * jt, LN), :].T

        def pack_rows(ref, src, f, p):
            for c in PLANES:
                SEND[f, p, 0, c] = ref[src, c, pl.ds(SB * (H + 2), H, stride=SB), :]
                high = ref[src, c, pl.ds(SB * 26 + 7, H, stride=SB), :]
                for m in range(H):
                    SEND[f, p, 1, c, m:m + 1, :] = high[11 - m:12 - m, :]

        def pack_cols(ref, src, f, p):
            for cp in PLANES:
                for c in PLANES:
                    blk = jnp.concatenate([ref[src, c, pl.ds(SB * (cp + 2) + s, 16, stride=24), :] for s in range(SB)], axis=0)
                    t = blk.T
                    for q in SIDES:
                        lo, hi = 3 * q + c, 3 * q + 2 - c
                        SEND[f, p, 2, cp, lo:lo + 1, :] = t[4 + q:5 + q, :]
                        SEND[f, p, 3, cp, hi:hi + 1, :] = t[123 - q:124 - q, :]

        def flip_and_sign(codes, f, p, winds):
            for side in SIDES:
                _, _, _, flip, turned, _ = codes[side]

                @pl.when(flip == 1)
                def _():
                    inside = lanes_of((NC * H, LN))
                    inside = jnp.logical_and(inside >= GL, inside < LN - GL)
                    old = jnp.concatenate([SEND[f, p, side, NC - 1 - c] for c in PLANES], axis=0)
                    mirror = (rows_of((LN, LN)) + lanes_of((LN, LN)) == LN - 1).astype(F32)
                    new = jnp.dot(jnp.where(inside, old, 0.0), mirror, precision=lax.Precision.HIGHEST,
                                  preferred_element_type=F32)
                    for c in PLANES:
                        SEND[f, p, side, c] = new[H * c:H * (c + 1)]
                if winds:
                    @pl.when(jnp.where(f == 1, turned, flip) == 1)
                    def _():
                        for c in PLANES:
                            SEND[f, p, side, c] = -SEND[f, p, side, c]

        def pack_corners(codes, f, p):
            lane = lanes_of((H, LN))
            for sa, sb in corners:
                _, _, _, side, x = corner_plan(codes, p, sa, sb)
                high = x == 1
                hi = lo = None
                for c in PLANES:
                    v = SEND[f, p, side, c]
                    vh, vl = pltpu.roll(v, SB + 4 * c, 1), pltpu.roll(v, 120 - 4 * c, 1)
                    hi = vh if c == 0 else jnp.where(lane >= 4 * c, vh, hi)
                    lo = vl if c == 0 else jnp.where(lane < LN - 4 * c, vl, lo)
                CSEND[f, p, 2 * sa + sb] = jnp.where(high, hi, lo)

        def start_copies(codes, f, fr, p):
            for side in SIDES:
                device, slot, dside, _ = dest(codes, p, side, 0)
                here = is_here(device)

                @pl.when(here)
                def _():
                    RECV[fr, slot, dside] = SEND[f, p, side]

                @pl.when(jnp.logical_not(here))
                def _():
                    pltpu.make_async_remote_copy(
                        src_ref=SEND.at[f, p, side], dst_ref=RECV.at[fr, slot, dside], send_sem=send_sem.at[f, p, side],
                        recv_sem=recv_sem.at[fr, slot, dside], device_id=device, device_id_type=mesh_ids).start()
            for sa, sb in corners:
                cid = 2 * sa + sb

                @pl.when(has_corner(sa, sb))
                def _():
                    device, slot, dcorner, _, _ = corner_plan(codes, p, sa, sb)
                    pltpu.make_async_remote_copy(
                        src_ref=CSEND.at[f, p, cid], dst_ref=CRECV.at[fr, slot, dcorner], send_sem=csend_sem.at[f, p, cid],
                        recv_sem=crecv_sem.at[fr, slot, dcorner], device_id=device, device_id_type=mesh_ids).start()

        def wait_copies(codes, strips, blocks, sem, csem, f, p):
            for side in SIDES:
                @pl.when(jnp.logical_not(is_here(dest(codes, p, side, 0)[0])))
                def _():
                    pltpu.make_async_copy(strips.at[f, p, side], strips.at[f, p, side], sem.at[f, p, side]).wait()
            for sa, sb in corners:
                cid = 2 * sa + sb

                @pl.when(has_corner(sa, sb))
                def _():
                    pltpu.make_async_copy(blocks.at[f, p, cid], blocks.at[f, p, cid], csem.at[f, p, cid]).wait()

        def end_valid(side, e):
            if side < 2:
                return jnp.logical_not(at_edge(2 + e))
            return jnp.logical_and(jnp.logical_not(at_edge(e)), at_edge(side))

        def merged(fr, p, side, c):
            lane = lanes_of((H, LN))
            v = RECV[fr, p, side, c]
            for e in range(2):
                cid = 2 * side + e if side < 2 else 2 * e + side - 2
                msg = CRECV[fr, p, cid]
                if c:
                    msg = pltpu.roll(msg, 4 * c if e else LN - 4 * c, 1)
                inside = lane >= 124 if e else lane < 4
                v = jnp.where(jnp.logical_and(inside, end_valid(side, e)), msg, v)
            return v

        def unpack_cols(ref, dst, fr, p):
            lane = lanes_of((16, LN))
            ghost = jnp.logical_or(lane < 4, lane >= 124)
            for cp in PLANES:
                low, high = merged(fr, p, 2, cp), merged(fr, p, 3, cp)
                for c in PLANES:
                    z = ZS.at[3 * cp + c]
                    for l in SIDES:
                        m = 3 * (3 - l) + 2 - c
                        z[l:l + 1, :] = low[m:m + 1, :]
                        m = 3 * l + c
                        z[124 + l:125 + l, :] = high[m:m + 1, :]
                    t = z[...].T
                    for s in range(SB):
                        rows = pl.ds(SB * (cp + 2) + s, 16, stride=24)
                        ref[dst, c, rows, :] = jnp.where(ghost, t[16 * s:16 * s + 16, :], ref[dst, c, rows, :])

        def unpack_rows(ref, dst, fr, p):
            lane = lanes_of((H, LN))
            keep = jnp.logical_and(jnp.logical_or(lane >= 4, end_valid(0, 0)), jnp.logical_or(lane < 124, end_valid(0, 1)))
            for c in PLANES:
                v = merged(fr, p, 0, c)
                for m in range(H):
                    row = pl.ds(SB * (13 - m), 1)
                    ref[dst, c, row, :] = jnp.where(keep[m:m + 1, :], v[m:m + 1, :], ref[dst, c, row, :])
                rows = pl.ds(SB * 38 + 7, H, stride=SB)
                ref[dst, c, rows, :] = jnp.where(keep, merged(fr, p, 1, c), ref[dst, c, rows, :])

        def pad_rows(ref):
            for p in range(NPAN):
                ref[p, :, pl.ds(0, 2 * SB), :] = ref[p, :, pl.ds(SB * KR - 1, 2 * SB), :]
                ref[p, :, pl.ds(SB * (KR + 2), 2 * SB), :] = ref[p, :, pl.ds(2 * SB + 1, 2 * SB), :]

        def corner_case(fn):
            for sa, sb in corners:
                @pl.when(jnp.logical_and(at_edge(sa), at_edge(2 + sb)))
                def _():
                    fn(sa, sb)

        def quad_geom(sa, sb):
            k0, s = (0, 0) if sa == 0 else (KR - H, SB - 1)
            lane0 = 0 if sb == 0 else LN - GL
            lane, idx = lanes_of((H, LN)), rows_of((H, LN))
            col = idx if sa == sb else H - 1 - idx
            masks = [NC * (lane - lane0) + c == col for c in PLANES]
            return k0, s, lane, masks, pl.ds(SB * (k0 + 2) + s, H, stride=SB)

        def beta_column(ref, src, sa, sb, r):
            k0, s, lane, masks, rows = quad_geom(sa, sb)
            kr = H + r if sa == 0 else KR - H - 1 - r
            tot = jnp.zeros((H, LN), F32)
            for c in PLANES:
                tot = jnp.where(masks[c], ref[src, c, pl.ds(SB * (kr + 2) + s, 1), :], tot)
            l_to, c_to = (GL - 1, NC - 1 - r) if sb == 0 else (LN - GL, r)
            return jnp.sum(tot, axis=1, keepdims=True), lane == l_to, c_to, rows

        def alpha_lines(ref, src, sa, sb, r):
            _, _, lane, masks, rows = quad_geom(sa, sb)
            l_from, c_from = (GL, r) if sb == 0 else (LN - GL - 1, NC - 1 - r)
            col = jnp.sum(jnp.where(lane == l_from, ref[src, c_from, rows, :], 0.0), axis=1, keepdims=True)
            return [jnp.sum(jnp.where(mask, col, 0.0), axis=0, keepdims=True) for mask in masks]

        def fill_quadrant(src, sa, sb):
            jobs = [(p, r) for p in range(NPAN) for r in range(2)]
            columns = [beta_column(src, p, sa, sb, r) for p, r in jobs]
            lines = [alpha_lines(src, p, sa, sb, r) for p, r in jobs]
            for (p, r), (col, mask, c_to, rows), line in zip(jobs, columns, lines):
                src[p, c_to, rows, :] = jnp.where(mask, col, src[p, c_to, rows, :])
                for c in PLANES:
                    CQ[p, r, c] = jnp.broadcast_to(line[c], (SB, LN))

        def fill_winds(sa, sb):
            sign = -1.0 if sa == sb else 1.0
            for p in range(NPAN):
                col, mask, c_to, rows = beta_column(WW, WA + p, sa, sb, 0)
                line = alpha_lines(WW, WB + p, sa, sb, 0)
                WW[WB + p, c_to, rows, :] = jnp.where(mask, sign * col, WW[WB + p, c_to, rows, :])
                row_lane = lanes_of((1, LN))
                inside = row_lane < GL if sb == 0 else row_lane >= LN - GL
                row = pl.ds(SB * (H + 1), 1) if sa == 0 else pl.ds(SB * (KR - H + 3) - 1, 1)
                for c in PLANES:
                    WW[WA + p, c, row, :] = jnp.where(inside, sign * line[c], WW[WA + p, c, row, :])

        def roll_down(v):
            return pltpu.roll(v, LN - 1, 1)

        def roll_up(v):
            return pltpu.roll(v, 1, 1)

        def beta_rows(src, p, k0, scale):
            rows = pl.ds(SB * (k0 + 2), SB * BETA_ROWS)
            a0, a1, a2 = (src[p, c, rows, :] for c in PLANES)
            a2l, a0r, a1r = roll_up(a2), roll_down(a0), roll_down(a1)
            e0, e1, e2 = a2l + a1, a0 + a2, a1 + a0r
            g0, g1, g2 = 8.0 * a0 - e0, 8.0 * a1 - e1, 8.0 * a2 - e2
            g0r = 8.0 * a0r - (a2 + a1r)
            x0 = WW[WB + p, 0, rows, :] * (g0 + g1)
            x1 = WW[WB + p, 1, rows, :] * (g1 + g2)
            x2 = WW[WB + p, 2, rows, :] * (g2 + g0r)
            x2l = roll_up(x2)
            return scale * (x0 - x2l) - e0, scale * (x1 - x0) - e1, scale * (x2 - x1) - e2

        def row_group(ref, p, k):
            return ref[p, :, pl.ds(SB * (k + 2), SB), :]

        def panel_pass(src, dst, p, scale, second):
            lane, sub = lanes_of((NC, SB, LN)), rows_of((NC, SB, LN))
            ghost_lane = jnp.logical_or(jnp.logical_and(at_edge(2), lane < GL),
                                        jnp.logical_and(at_edge(3), lane >= LN - GL))
            in_low = jnp.logical_and(ghost_lane, jnp.logical_and(at_edge(0), sub == 0))
            in_high = jnp.logical_and(ghost_lane, jnp.logical_and(at_edge(1), sub == SB - 1))

            def load(k):
                v = row_group(src, p, k)
                if k in (H - 2, H - 1):
                    return jnp.where(in_low, CQ[p, H - 1 - k], v)
                if k in (KR - H, KR - H + 1):
                    return jnp.where(in_high, CQ[p, k - (KR - H)], v)
                return v

            qm, q0, q1 = load(-2), load(-1), load(0)
            q2 = load(1)
            g0 = 8.0 * q0 - (qm + q1)
            e1 = q0 + q2
            g1 = 8.0 * q1 - e1
            x_low = row_group(WW, WA + p, -1) * (g0 + g1)
            q_now, e_now, g_now, q_next = q1, e1, g1, q2
            beta = None
            for k in range(KR):
                if k % BETA_ROWS == 0:
                    beta = beta_rows(src, p, k, scale)
                at = SB * (k % BETA_ROWS)
                tb = jnp.stack([beta[c][at:at + SB] for c in PLANES])
                q_far = load(k + 2)
                e_next = q_now + q_far
                g_next = 8.0 * q_next - e_next
                x_high = row_group(WW, WA + p, k) * (g_now + g_next)
                u = scale * (x_high - x_low) - e_now + tb + 4.0 * q_now
                new = q_now - KK[:, pl.ds(SB * k, SB), :] * u
                if second:
                    new = 0.5 * (row_group(dst, p, k) + new)
                dst[p, :, pl.ds(SB * (k + 2), SB), :] = new
                x_low, q_now, e_now, g_now, q_next = x_high, q_next, e_next, g_next, q_far

        def stage(src, dst, scale, second):
            pad_rows(src)
            corner_case(lambda sa, sb: fill_quadrant(src, sa, sb))

            @pl.loop(0, NPAN)
            def _(p):
                panel_pass(src, dst, p, scale, second)

        load_field(a_in, WW, WA)
        load_field(b_in, WW, WB)
        is_cc = jnp.logical_and(jnp.logical_or(at_edge(0), at_edge(1)), jnp.logical_or(at_edge(2), at_edge(3)))
        pl.semaphore_wait(barrier, SB * NPAN - NPAN * jnp.where(is_cc, 1, 0))

        @pl.loop(0, 2 * NPAN)
        def _(n):
            f, p = lax.div(n, NPAN) + 1, lax.rem(n, NPAN)
            codes = edge_codes(p)
            pack_rows(WW, n, f, p)
            pack_cols(WW, (2 - f) * NPAN + p, f, p)
            flip_and_sign(codes, f, p, True)
            pack_corners(codes, f, p)
            start_copies(codes, f, f + 1, p)
        load_field(q_in, QA, 0)

        def finish_winds():
            metric()

            @pl.loop(0, 2 * NPAN)
            def _(n):
                f, p = lax.div(n, NPAN) + 1, lax.rem(n, NPAN)
                wait_copies(edge_codes(p), RECV, CRECV, recv_sem, crecv_sem, f + 1, p)
                unpack_cols(WW, (2 - f) * NPAN + p, f + 1, p)

            @pl.loop(0, 2 * NPAN)
            def _(n):
                f, p = lax.div(n, NPAN) + 1, lax.rem(n, NPAN)
                unpack_rows(WW, n, f + 1, p)
                wait_copies(edge_codes(p), SEND, CSEND, send_sem, csend_sem, f, p)
            corner_case(fill_winds)
            pad_rows(WW)
            face_scale = 0.5 / (12.0 * 0.5 * C_SPEED)

            @pl.loop(0, NPAN)
            def _(p):
                for c in PLANES:
                    low, high = pl.ds(SB, SB * (KR + 1)), pl.ds(2 * SB, SB * (KR + 1))
                    WW[WA + p, c, low, :] = face_scale * (WW[WA + p, c, low, :] + WW[WA + p, c, high, :])
                rows = pl.ds(2 * SB, SB * KR)
                b0, b1, b2 = (WW[WB + p, c, rows, :] for c in PLANES)
                WW[WB + p, 0, rows, :] = face_scale * (b0 + b1)
                WW[WB + p, 1, rows, :] = face_scale * (b1 + b2)
                WW[WB + p, 2, rows, :] = face_scale * (b2 + roll_down(b0))

        def metric():
            ridx = rows_of((SB * KR, LN))
            gi = tx * tile_rows + lax.rem(ridx, SB) * KR + lax.div(ridx, SB) - H
            gi = jnp.where(gi < 0, -1 - gi, jnp.where(gi >= cells, 2 * cells - 1 - gi, gi))
            tan_a = small_tan((gi.astype(F32) + 0.5) * dalpha - 0.25 * math.pi)
            for c in PLANES:
                gj = ty * tile_rows + 3 * lanes_of((SB, LN)) + c - H
                gj = jnp.where(gj < 0, -1 - gj, jnp.where(gj >= cells, 2 * cells - 1 - gj, gj))
                tan_b = small_tan((gj.astype(F32) + 0.5) * dalpha - 0.25 * math.pi)[0:1, :]
                a_sq, b_sq = tan_a * tan_a, tan_b * tan_b
                r_sq = 1.0 + a_sq + b_sq
                sqrt_g = (1.0 + a_sq) * (1.0 + b_sq) / (r_sq * jnp.sqrt(r_sq))
                KK[c] = (0.5 * C_SPEED * CFL_STEP) / sqrt_g

        @pl.loop(0, n_blocks)
        def _(b):
            fr = lax.rem(b, 2)

            @pl.loop(0, NPAN)
            def _(p):
                codes = edge_codes(p)
                pack_rows(QA, p, 0, p)
                pack_cols(QA, p, 0, p)
                flip_and_sign(codes, 0, p, False)
                pack_corners(codes, 0, p)
                start_copies(codes, 0, fr, p)

            @pl.when(b == 0)
            def _():
                finish_winds()

            @pl.loop(0, NPAN)
            def _(p):
                codes = edge_codes(p)
                wait_copies(codes, RECV, CRECV, recv_sem, crecv_sem, fr, p)
                unpack_cols(QA, p, fr, p)
                unpack_rows(QA, p, fr, p)
                wait_copies(codes, SEND, CSEND, send_sem, csend_sem, 0, p)

            @pl.loop(lax.div(b * steps, n_blocks), lax.div((b + 1) * steps, n_blocks))
            def _(t):
                scale = ws_ref[t]
                stage(QA, QB, scale, False)
                stage(QB, QA, scale, True)

        store_field(QA)

    return kernel


def solution(mesh):
    tile_count = mesh.shape['tx']
    field_spec = P(('member', 'panel'), 'tx', 'ty')
    wind_spec = P('panel', 'tx', 'ty')

    def local_run(tracer, wind_a, wind_b, wind_scale):
        steps = wind_scale.shape[0]
        n_blocks = -(-steps // STEPS_PER_BLOCK)
        ext = SB * KR
        block = pl.BlockSpec((NPAN, ext, ext), lambda n: (0, 0, 0))
        dma = pltpu.SemaphoreType.DMA
        return pl.pallas_call(
            make_kernel(tile_count, steps, n_blocks, tracer.shape[1]),
            grid=(1,),
            out_shape=jax.ShapeDtypeStruct(tracer.shape, F32),
            in_specs=[pl.BlockSpec(memory_space=pltpu.SMEM), block, block, block],
            out_specs=block,
            scratch_shapes=[
                pltpu.VMEM((NPAN, NC, ext + 32, LN), F32),
                pltpu.VMEM((NPAN, NC, ext + 32, LN), F32),
                pltpu.VMEM((2 * NPAN, NC, ext + 32, LN), F32),
                pltpu.VMEM((NPAN, 2, NC, SB, LN), F32),
                pltpu.VMEM((NC, ext, LN), F32),
                pltpu.VMEM((NC, ext + 32, LN), F32),
                pltpu.VMEM((NC, ext + 32, LN), F32),
                pltpu.VMEM((9, LN, LN), F32),
                pltpu.VMEM((3, NPAN, 4, NC, H, LN), F32),
                pltpu.VMEM((4, NPAN, 4, NC, H, LN), F32),
                pltpu.VMEM((3, NPAN, 4, H, LN), F32),
                pltpu.VMEM((4, NPAN, 4, H, LN), F32),
                *[dma((n, NPAN, 4)) for n in (3, 4, 3, 4)],
            ],
            compiler_params=pltpu.CompilerParams(collective_id=0, has_side_effects=True, vmem_limit_bytes=60 * 1024 * 1024),
            cost_estimate=pl.CostEstimate(flops=10 ** 9, bytes_accessed=10 ** 7, transcendentals=0),
        )(wind_scale, tracer, wind_a, wind_b)

    return jax.shard_map(local_run, mesh=mesh, in_specs=(field_spec, wind_spec, wind_spec, P()),
                         out_specs=field_spec, check_vma=False)
```

time: 2890 us -> 134 us (0.05); the launches traced: 2860 us -> 134 us
  starting transfers between devices: 1680 us -> 0 us
  waiting for transfers between devices: 460 us -> 0 us
  local copies, waits for them, and re-layouts: 358 us -> 2.72 us
  other arithmetic: 339 us -> 0 us
  Pallas kernels: 0 us -> 132 us
    ppermute x924 -> x0, starting transfers between devices: 1680 us -> none  [the longest x792 1420 us: fill_halo(): moved_strip = lax.ppermute(one_strip, group_axes, perm_pairs)]
    ppermute x924 -> x0, waiting for transfers between devices: 460 us -> none  [the longest x792 419 us: fill_halo(): moved_strip = lax.ppermute(one_strip, group_axes, perm_pairs)]
    sub x64 -> x0, other arithmetic: 225 us -> none  [face_flux_div(): step_scale * wind_face * face_val - 0.5 * C_SPEED * (near_right - near_left)]
    while x592 -> x0, local copies, waits for them, and re-layouts: 136 us -> none
    pallas_call x0 -> x1, Pallas kernels: none -> 132 us  [local_run(): pl.pallas_call(make_kernel(tile_count, steps, n_blocks, tracer.shape[1]),...]
    rev x99 -> x0, local copies, waits for them, and re-layouts: 100 us -> none  [the longest x33 91.5 us: to_blocks(): jnp.flip(ghosts[2], axis=1)]
    add x149 -> x0, other arithmetic: 66.9 us -> none  [the longest x132 55.6 us: fill_halo(): own_blk + cross_blk]
    ppermute x32 -> x0, local copies, waits for them, and re-layouts: 34 us -> none  [the longest x16 17 us: fill_halo(): lax.ppermute(field_b[:, :, -2:], 'ty', shift_up)]
  transfers between devices with their start and end apart: 924 -> 0, of which waited for: 97 -> 0; matrix products, arithmetic and copies ran while one was open for 19% -> 0% of each run, Pallas kernels for 0% -> 0%
where the time goes in v1:
time: 134 us
  Pallas kernels  132 us (99%)
  local copies, waits for them, and re-layouts  2.72 us (2%)
    pallas_call x1, Pallas kernels, local_run(): pl.pallas_call(make_kernel(tile_count, steps, n_blocks, tracer.shape[1]),...  132 us
    unnamed x1, local copies, waits for them, and re-layouts  2.72 us

profile of v1, /device:TPU:97, one launch (start us, length us, event | category | flops | bytes accessed | tf_op | source)
XLA Modules:
  0.0 134.3 jit_solution(12837848835661988707)
XLA Ops:
  0.0 131.6 %shard_map.46 = f32[3,360,360]{2,1,0:T(8,128)} custom-call(f32[16]{0:T(128)} %ws_ref.1, f32[3,360,360]{2,1,0:T(8,128)} %q_in.1, f32[3,360,360]{2,1,0:T(8,128)} %a_in.1, f32[3,360,360]{2,1,0:T(8,128)} %b_in.1), custom_call_target="tpu_custom_call" | custom-call | flops 1000000000 | bytes 10000000 | tf_op jit(solution)/shard_map/pallas_call | solution.py:519
  131.6 2.7 %copy.6 = f32[3,360,360]{2,1,0:T(8,128)} copy(f32[3,360,360]{2,1,0:T(8,128)} %shard_map.46) | data formatting | bytes 3110400

commit v2 on v1

v2 whole, which is shorter than its diff:
```python
import math
import jax
import numpy as np
import jax.numpy as jnp
from jax import lax
from jax.experimental import pallas as pl
from jax.experimental.pallas import tpu as pltpu
from jax.sharding import PartitionSpec as P

C_SPEED = 2.5
CFL_STEP = 0.12
EDGE_CODE = (
    (310, 100, 530, 420), (10, 200, 511, 410), (110, 300, 521, 431),
    (210, 0, 500, 401), (331, 130, 30, 231), (320, 121, 221, 20),
)
H = 12
KR = 48
NPAN = 3
NC = 3
SB = 8
LN = 128
GL = 4
STEPS_PER_BLOCK = 3
BETA_ROWS = 4
F32 = jnp.float32
PLANES = range(NC)
SIDES = range(4)


def turned_sign(side_id, edge_id):
    return int(side_id % 2 == edge_id % 2)


def small_tan(v):
    sq = v * v
    sin_sum, cos_sum = jnp.full_like(v, 1.0), jnp.full_like(v, 1.0)
    for n in (6, 5, 4, 3, 2, 1):
        sin_sum = 1.0 - sq * sin_sum * (1.0 / (2 * n * (2 * n + 1)))
        cos_sum = 1.0 - sq * cos_sum * (1.0 / (2 * n * (2 * n - 1)))
    return v * sin_sum / cos_sum


def sel(pred, yes, no):
    yes, no = (np.int32(v) if isinstance(v, int) else v for v in (yes, no))
    same = jnp.shape(yes) == jnp.shape(no) and jnp.shape(pred) in ((), jnp.shape(yes))
    return lax.select(pred, yes, no) if same else jnp.where(pred, yes, no)


def lanes_of(shape):
    return lax.broadcasted_iota(jnp.int32, shape, len(shape) - 1)


def rows_of(shape):
    return lax.broadcasted_iota(jnp.int32, shape, len(shape) - 2)


def make_kernel(tile_count, steps, n_blocks, tile_rows):
    last = tile_count - 1
    cells = tile_rows * tile_count
    dalpha = 0.5 * math.pi / cells

    def kernel(ws_ref, q_in, a_in, b_in, out_ref, QA, QB, WW, CQ, KK, NN, TT, ZS, SEND, RECV, CSEND, CRECV,
               send_sem, recv_sem, csend_sem, crecv_sem):
        dev = lax.axis_index('panel')
        tx = lax.axis_index('tx')
        ty = lax.axis_index('ty')
        WA, WB = 0, NPAN

        def at_edge(side):
            return (tx == 0, tx == last, ty == 0, ty == last)[side]

        def pick(v0, v1):
            return v0 if v0 == v1 else v0 + dev * (v1 - v0)

        def neighbour(p, side):
            codes = [EDGE_CODE[NPAN * dv + p][side] for dv in (0, 1)]
            panels = [code // 100 for code in codes]
            edges = [code // 10 % 10 for code in codes]
            return (pick(*[n // NPAN for n in panels]), pick(*[n % NPAN for n in panels]), pick(*edges),
                    pick(*[code % 10 for code in codes]), pick(*[turned_sign(side, e) for e in edges]))

        def dest(p, side, off):
            along = (ty if side < 2 else tx) + off
            edge = at_edge(side)
            d_dev, d_slot, dside, flip, _ = neighbour(p, side)
            al = along + flip * (last - 2 * along)
            c_tx = sel(dside == 0, 0, sel(dside == 1, last, al))
            c_ty = sel(dside == 2, 0, sel(dside == 3, last, al))
            step = 2 * (side % 2) - 1
            in_tx, in_ty = (tx + step, ty + off) if side < 2 else (tx + off, ty + step)
            device = {'tx': sel(edge, c_tx, in_tx), 'ty': sel(edge, c_ty, in_ty),
                      'panel': sel(edge, d_dev, dev)}
            return device, sel(edge, d_slot, p), sel(edge, dside, side ^ 1), sel(edge, flip, 0)

        def corner_plan(p, sa, sb):
            out_b = at_edge(2 + sb)
            plans = []
            for side, end, off in ((sa, sb, 2 * sb - 1), (2 + sb, sa, 2 * sa - 1)):
                device, slot, dside, flip = dest(p, side, off)
                x = end + flip * (1 - 2 * end)
                e = 1 - x
                plans.append((device, slot, sel(dside < 2, 2 * dside + e, 2 * e + (dside - 2)), side, x))
            (dv_a, sl_a, dc_a, s_a, x_a), (dv_b, sl_b, dc_b, s_b, x_b) = plans
            device = {key: sel(out_b, dv_b[key], dv_a[key]) for key in dv_a}
            return (device, sel(out_b, sl_b, sl_a), sel(out_b, dc_b, dc_a),
                    sel(out_b, s_b, s_a), sel(out_b, x_b, x_a))

        def has_corner(sa, sb):
            return jnp.logical_not(jnp.logical_and(at_edge(sa), at_edge(2 + sb)))

        def is_here(device):
            return jnp.logical_and(jnp.logical_and(device['tx'] == tx, device['ty'] == ty), device['panel'] == dev)

        corners = [(sa, sb) for sa in range(2) for sb in range(2)]
        slots = range(NPAN)
        strip_to = [[dest(p, side, 0)[:3] for side in SIDES] for p in slots]
        stays = [[is_here(plan[0]) for plan in row] for row in strip_to]
        corner_to = [[corner_plan(p, sa, sb) for sa, sb in corners] for p in slots]
        mesh_ids = pl.DeviceIdType.MESH

        barrier = pltpu.get_barrier_semaphore()

        for p in slots:
            for side in SIDES:
                pl.semaphore_signal(barrier, inc=1, device_id=strip_to[p][side][0], device_id_type=mesh_ids)
            for (sa, sb), plan in zip(corners, corner_to[p]):
                @pl.when(has_corner(sa, sb))
                def _():
                    pl.semaphore_signal(barrier, inc=1, device_id=plan[0], device_id_type=mesh_ids)

        def load_field(in_ref, dst, base):
            @pl.loop(0, NPAN)
            def _(p):
                for it in PLANES:
                    for jt in PLANES:
                        TT[it, pl.ds(H + LN * jt, LN), :] = in_ref[p, pl.ds(LN * it, LN), pl.ds(LN * jt, LN)].T
                    for c in PLANES:
                        NN[c, pl.ds(H + LN * it, LN), :] = TT[it, pl.ds(c, LN, stride=NC), :].T

                @pl.loop(0, KR // SB)
                def _(kb):
                    for c in PLANES:
                        for k in range(SB):
                            dst[base + p, c, pl.ds(pl.multiple_of(64 * kb + SB * (k + 2), SB), SB), :] = NN[c, pl.ds(SB * kb + k, SB, stride=KR), :]

        def store_field(src):
            @pl.loop(0, NPAN)
            def _(p):
                @pl.loop(0, KR // SB)
                def _(kb):
                    for c in PLANES:
                        for k in range(SB):
                            NN[c, pl.ds(SB * kb + k, SB, stride=KR), :] = src[p, c, pl.ds(pl.multiple_of(64 * kb + SB * (k + 2), SB), SB), :]
                for it in PLANES:
                    for c in PLANES:
                        TT[it, pl.ds(c, LN, stride=NC), :] = NN[c, pl.ds(H + LN * it, LN), :].T
                    for jt in PLANES:
                        out_ref[p, pl.ds(LN * it, LN), pl.ds(LN * jt, LN)] = TT[it, pl.ds(H + LN * jt, LN), :].T

        def quarter(n):
            return pl.ds(GL * n, GL)

        def rows_at(first, s, n):
            return pl.ds(SB * (first + 2 + n) + s, GL, stride=NC * SB)

        def pack_strips(row_ref, row_at, col_ref, col_at, f, p):
            for c in PLANES:
                for n in PLANES:
                    SEND[f, p, 0, c, quarter(n), :] = row_ref[row_at, c, rows_at(H, 0, n), :]
                    SEND[f, p, 1, c, quarter(n), :] = row_ref[row_at, c, rows_at(KR - 2 * H, SB - 1, n), :]
            lane = lanes_of((LN, LN))

            def window(first):
                return jnp.logical_and(lane >= first, lane < first + GL)
            for cp in PLANES:
                mix = None
                for c in PLANES:
                    blk = jnp.concatenate([col_ref[col_at, c, pl.ds(SB * (cp + 2) + s, 2 * SB, stride=NC * SB), :]
                                           for s in range(SB)], axis=0)
                    if c == 0:
                        mix = blk
                    else:
                        mine = jnp.logical_or(window(GL + SB * c), window(SB * (c - 1)))
                        mix = sel(mine, pltpu.roll(blk, SB * c, 1), mix)
                t = mix.T
                for c in PLANES:
                    low, high = GL + SB * c, (LN - SB + SB * c) % LN
                    SEND[f, p, 2, cp, quarter(c), :] = t[low:low + GL]
                    SEND[f, p, 3, cp, quarter(c), :] = t[high:high + GL]

        def turn_strips(f, p, winds):
            for side in SIDES:
                _, _, _, flip, turned = neighbour(p, side)
                if not isinstance(flip, int) or flip:
                    @pl.when(sel(at_edge(side), flip, 0) == 1)
                    def _():
                        inside = lanes_of((NC * H, LN))
                        inside = jnp.logical_and(inside >= GL, inside < LN - GL)
                        old = jnp.concatenate([SEND[f, p, side, NC - 1 - c] for c in PLANES], axis=0)
                        mirror = (rows_of((LN, LN)) + lanes_of((LN, LN)) == LN - 1).astype(F32)
                        new = jnp.dot(sel(inside, old, 0.0), mirror, precision=lax.Precision.HIGHEST,
                                      preferred_element_type=F32)
                        for c in PLANES:
                            SEND[f, p, side, c] = new[H * c:H * (c + 1)]
                        if winds:
                            @pl.when(f == 2)
                            def _():
                                for c in PLANES:
                                    SEND[f, p, side, c] = -SEND[f, p, side, c]
                if not isinstance(turned, int) or turned:
                    @pl.when(sel(at_edge(side), turned, 0) == 1)
                    def _():
                        for c in PLANES:
                            v = SEND[f, p, side, c]
                            if winds:
                                v = sel(f == 1, -v, v)
                            for m in range(H):
                                SEND[f, p, side, c, m:m + 1, :] = v[H - 1 - m:H - m, :]

        def pack_corners(f, p):
            lane = lanes_of((H, LN))
            for cid, (_, _, _, side, x) in enumerate(corner_to[p]):
                hi = lo = None
                for c in PLANES:
                    v = SEND[f, p, side, c]
                    vh, vl = pltpu.roll(v, SB + GL * c, 1), pltpu.roll(v, LN - SB - GL * c, 1)
                    hi = vh if c == 0 else sel(lane >= GL * c, vh, hi)
                    lo = vl if c == 0 else sel(lane < LN - GL * c, vl, lo)
                CSEND[f, p, cid] = sel(x == 1, hi, lo)

        def start_copies(f, fr, p):
            for side in SIDES:
                device, slot, dside = strip_to[p][side]
                here = stays[p][side]

                @pl.when(here)
                def _():
                    RECV[fr, slot, dside] = SEND[f, p, side]

                @pl.when(jnp.logical_not(here))
                def _():
                    pltpu.make_async_remote_copy(
                        src_ref=SEND.at[f, p, side], dst_ref=RECV.at[fr, slot, dside], send_sem=send_sem.at[f, p, side],
                        recv_sem=recv_sem.at[fr, slot, dside], device_id=device, device_id_type=mesh_ids).start()
            for cid, (sa, sb) in enumerate(corners):
                @pl.when(has_corner(sa, sb))
                def _():
                    device, slot, dcorner, _, _ = corner_to[p][cid]
                    pltpu.make_async_remote_copy(
                        src_ref=CSEND.at[f, p, cid], dst_ref=CRECV.at[fr, slot, dcorner], send_sem=csend_sem.at[f, p, cid],
                        recv_sem=crecv_sem.at[fr, slot, dcorner], device_id=device, device_id_type=mesh_ids).start()

        def wait_copies(strips, blocks, sem, csem, f, p):
            for side in SIDES:
                @pl.when(jnp.logical_not(stays[p][side]))
                def _():
                    pltpu.make_async_copy(strips.at[f, p, side], strips.at[f, p, side], sem.at[f, p, side]).wait()
            for cid, (sa, sb) in enumerate(corners):
                @pl.when(has_corner(sa, sb))
                def _():
                    pltpu.make_async_copy(blocks.at[f, p, cid], blocks.at[f, p, cid], csem.at[f, p, cid]).wait()

        def end_valid(side, e):
            if side < 2:
                return jnp.logical_not(at_edge(2 + e))
            return jnp.logical_and(jnp.logical_not(at_edge(e)), at_edge(side))

        def merged(fr, p, side, c):
            lane = lanes_of((H, LN))
            v = RECV[fr, p, side, c]
            for e in range(2):
                cid = 2 * side + e if side < 2 else 2 * e + side - 2
                msg = CRECV[fr, p, cid]
                if c:
                    msg = pltpu.roll(msg, 4 * c if e else LN - 4 * c, 1)
                inside = lane >= 124 if e else lane < 4
                v = sel(jnp.logical_and(inside, end_valid(side, e)), msg, v)
            return v

        def unpack_cols(ref, dst, fr, p):
            lane = lanes_of((2 * SB, LN))
            ghost = jnp.logical_or(lane < GL, lane >= LN - GL)
            for cp in PLANES:
                low, high = merged(fr, p, 2, cp), merged(fr, p, 3, cp)
                z = ZS.at[NC * p + cp]
                for c in PLANES:
                    z[pl.ds(SB * c, GL), :] = low[GL * c:GL * (c + 1)]
                    z[pl.ds((SB * c - GL) % LN, GL), :] = high[GL * c:GL * (c + 1)]
                t = z[...].T
                for c in PLANES:
                    tc = pltpu.roll(t, LN - SB * c, 1) if c else t
                    for s in range(SB):
                        rows = pl.ds(SB * (cp + 2) + s, 2 * SB, stride=NC * SB)
                        ref[dst, c, rows, :] = sel(ghost, tc[2 * SB * s:2 * SB * (s + 1)], ref[dst, c, rows, :])

        def unpack_rows(ref, dst, fr, p):
            lane = lanes_of((GL, LN))
            keep = jnp.logical_and(jnp.logical_or(lane >= GL, end_valid(0, 0)),
                                   jnp.logical_or(lane < LN - GL, end_valid(0, 1)))
            for c in PLANES:
                for side, first, s in ((0, 0, 0), (1, KR - H, SB - 1)):
                    v = merged(fr, p, side, c)
                    for n in PLANES:
                        rows = rows_at(first, s, n)
                        ref[dst, c, rows, :] = sel(keep, v[GL * n:GL * (n + 1)], ref[dst, c, rows, :])

        def pad_rows(ref):
            at = pl.ds(0, NPAN)
            ref[at, :, pl.ds(0, 2 * SB), :] = ref[at, :, pl.ds(SB * KR - 1, 2 * SB), :]
            ref[at, :, pl.ds(SB * (KR + 2), 2 * SB), :] = ref[at, :, pl.ds(2 * SB + 1, 2 * SB), :]

        def corner_case(fn):
            for sa, sb in corners:
                @pl.when(jnp.logical_and(at_edge(sa), at_edge(2 + sb)))
                def _():
                    fn(sa, sb)

        def quad_geom(sa, sb):
            k0, s = (0, 0) if sa == 0 else (KR - H, SB - 1)
            lane0 = 0 if sb == 0 else LN - GL
            lane, idx = lanes_of((H, LN)), rows_of((H, LN))
            col = idx if sa == sb else H - 1 - idx
            masks = [NC * (lane - lane0) + c == col for c in PLANES]
            return k0, s, lane, masks, pl.ds(SB * (k0 + 2) + s, H, stride=SB)

        def beta_column(ref, first, sa, sb, r):
            k0, s, lane, masks, rows = quad_geom(sa, sb)
            kr = H + r if sa == 0 else KR - H - 1 - r
            tot = jnp.zeros((NPAN, H, LN), F32)
            for c in PLANES:
                line = ref[pl.ds(first, NPAN), c, pl.ds(SB * (kr + 2) + s, 1), :]
                tot = sel(wide(masks[c]), jnp.broadcast_to(line, tot.shape), tot)
            l_to, c_to = (GL - 1, NC - 1 - r) if sb == 0 else (LN - GL, r)
            return jnp.broadcast_to(jnp.sum(tot, axis=2, keepdims=True), tot.shape), wide(lane == l_to), c_to, rows

        def alpha_lines(ref, first, sa, sb, r):
            _, _, lane, masks, rows = quad_geom(sa, sb)
            l_from, c_from = (GL, r) if sb == 0 else (LN - GL - 1, NC - 1 - r)
            zero = jnp.zeros((NPAN, H, LN), F32)
            col = jnp.sum(sel(wide(lane == l_from), ref[pl.ds(first, NPAN), c_from, rows, :], zero), axis=2, keepdims=True)
            col = jnp.broadcast_to(col, zero.shape)
            return [jnp.sum(sel(wide(mask), col, zero), axis=1, keepdims=True) for mask in masks]

        def wide(mask):
            return jnp.broadcast_to(mask[None], (NPAN, *mask.shape))

        def fill_quadrant(src, sa, sb):
            columns = [beta_column(src, 0, sa, sb, r) for r in range(2)]
            lines = [alpha_lines(src, 0, sa, sb, r) for r in range(2)]
            for r in range(2):
                col, mask, c_to, rows = columns[r]
                src[:, c_to, rows, :] = sel(mask, col, src[:, c_to, rows, :])
                for c in PLANES:
                    CQ[:, r, c] = jnp.broadcast_to(lines[r][c], (NPAN, SB, LN))

        def fill_winds(sa, sb):
            sign = -1.0 if sa == sb else 1.0
            col, mask, c_to, rows = beta_column(WW, WA, sa, sb, 0)
            line = alpha_lines(WW, WB, sa, sb, 0)
            to_b, to_a = pl.ds(WB, NPAN), pl.ds(WA, NPAN)
            WW[to_b, c_to, rows, :] = sel(mask, sign * col, WW[to_b, c_to, rows, :])
            row_lane = lanes_of((NPAN, 1, LN))
            inside = row_lane < GL if sb == 0 else row_lane >= LN - GL
            row = pl.ds(SB * (H + 1), 1) if sa == 0 else pl.ds(SB * (KR - H + 3) - 1, 1)
            for c in PLANES:
                WW[to_a, c, row, :] = sel(inside, sign * line[c], WW[to_a, c, row, :])

        def roll_down(v):
            return pltpu.roll(v, LN - 1, 1)

        def roll_up(v):
            return pltpu.roll(v, 1, 1)

        def beta_rows(src, p, k0, scale):
            rows = pl.ds(SB * (k0 + 2), SB * BETA_ROWS)
            a0, a1, a2 = (src[p, c, rows, :] for c in PLANES)
            a2l, a0r, a1r = roll_up(a2), roll_down(a0), roll_down(a1)
            e0, e1, e2 = a2l + a1, a0 + a2, a1 + a0r
            g0, g1, g2 = 8.0 * a0 - e0, 8.0 * a1 - e1, 8.0 * a2 - e2
            g0r = 8.0 * a0r - (a2 + a1r)
            x0 = WW[WB + p, 0, rows, :] * (g0 + g1)
            x1 = WW[WB + p, 1, rows, :] * (g1 + g2)
            x2 = WW[WB + p, 2, rows, :] * (g2 + g0r)
            x2l = roll_up(x2)
            return jnp.stack([x0 - x2l, x1 - x0, x2 - x1]), jnp.stack([e0, e1, e2])

        def row_group(ref, p, k):
            return ref[p, :, pl.ds(SB * (k + 2), SB), :]

        def panel_pass(src, dst, p, scale, second):
            lane, sub = lanes_of((NC, SB, LN)), rows_of((NC, SB, LN))
            ghost_lane = jnp.logical_or(jnp.logical_and(at_edge(2), lane < GL),
                                        jnp.logical_and(at_edge(3), lane >= LN - GL))
            in_low = jnp.logical_and(ghost_lane, jnp.logical_and(at_edge(0), sub == 0))
            in_high = jnp.logical_and(ghost_lane, jnp.logical_and(at_edge(1), sub == SB - 1))

            def load(k):
                v = row_group(src, p, k)
                if k in (H - 2, H - 1):
                    return sel(in_low, CQ[p, H - 1 - k], v)
                if k in (KR - H, KR - H + 1):
                    return sel(in_high, CQ[p, k - (KR - H)], v)
                return v

            qm, q0, q1 = load(-2), load(-1), load(0)
            q2 = load(1)
            g0 = 8.0 * q0 - (qm + q1)
            e1 = q0 + q2
            g1 = 8.0 * q1 - e1
            x_low = row_group(WW, WA + p, -1) * (g0 + g1)
            q_now, e_now, g_now, q_next = q1, e1, g1, q2
            beta = None
            for k in range(KR):
                if k % BETA_ROWS == 0:
                    beta = beta_rows(src, p, k, scale)
                at = SB * (k % BETA_ROWS)
                tb, eb = (v[:, at:at + SB] for v in beta)
                q_far = load(k + 2)
                e_next = q_now + q_far
                g_next = 8.0 * q_next - e_next
                x_high = row_group(WW, WA + p, k) * (g_now + g_next)
                u = scale * (x_high - x_low + tb) - (e_now + eb)
                new = KK[1, :, pl.ds(SB * k, SB), :] * q_now - KK[0, :, pl.ds(SB * k, SB), :] * u
                if second:
                    new = 0.5 * (row_group(dst, p, k) + new)
                dst[p, :, pl.ds(SB * (k + 2), SB), :] = new
                x_low, q_now, e_now, g_now, q_next = x_high, q_next, e_next, g_next, q_far

        def stage(src, dst, scale, second, more):
            pad_rows(src)

            @pl.when(more)
            def _():
                corner_case(lambda sa, sb: fill_quadrant(src, sa, sb))

            @pl.loop(0, NPAN)
            def _(p):
                panel_pass(src, dst, p, scale, second)

        load_field(a_in, WW, WA)
        load_field(b_in, WW, WB)
        is_cc = jnp.logical_and(jnp.logical_or(at_edge(0), at_edge(1)), jnp.logical_or(at_edge(2), at_edge(3)))
        pl.semaphore_wait(barrier, SB * NPAN - NPAN * sel(is_cc, 1, 0))

        @pl.loop(1, 3)
        def _(f):
            @pl.loop(0, NPAN)
            def _(p):
                pack_strips(WW, (f - 1) * NPAN + p, WW, (2 - f) * NPAN + p, f, p)
            for p in slots:
                turn_strips(f, p, True)
            for p in slots:
                pack_corners(f, p)
            for p in slots:
                start_copies(f, f + 1, p)
        load_field(q_in, QA, 0)

        def finish_winds():
            metric()

            @pl.loop(1, 3)
            def _(f):
                for p in slots:
                    wait_copies(RECV, CRECV, recv_sem, crecv_sem, f + 1, p)

                @pl.loop(0, NPAN)
                def _(p):
                    unpack_cols(WW, (2 - f) * NPAN + p, f + 1, p)

            @pl.loop(1, 3)
            def _(f):
                @pl.loop(0, NPAN)
                def _(p):
                    unpack_rows(WW, (f - 1) * NPAN + p, f + 1, p)
                for p in slots:
                    wait_copies(SEND, CSEND, send_sem, csend_sem, f, p)
            corner_case(fill_winds)
            pad_rows(WW)
            face_scale = 0.5 / (12.0 * 0.5 * C_SPEED)

            @pl.loop(0, NPAN)
            def _(p):
                for c in PLANES:
                    low, high = pl.ds(SB, SB * (KR + 1)), pl.ds(2 * SB, SB * (KR + 1))
                    WW[WA + p, c, low, :] = face_scale * (WW[WA + p, c, low, :] + WW[WA + p, c, high, :])
                rows = pl.ds(2 * SB, SB * KR)
                b0, b1, b2 = (WW[WB + p, c, rows, :] for c in PLANES)
                WW[WB + p, 0, rows, :] = face_scale * (b0 + b1)
                WW[WB + p, 1, rows, :] = face_scale * (b1 + b2)
                WW[WB + p, 2, rows, :] = face_scale * (b2 + roll_down(b0))

        def metric():
            ridx = rows_of((SB * KR, LN))
            gi = tx * tile_rows + lax.rem(ridx, SB) * KR + lax.div(ridx, SB) - H
            gi = sel(gi < 0, -1 - gi, sel(gi >= cells, 2 * cells - 1 - gi, gi))
            tan_a = small_tan((gi.astype(F32) + 0.5) * dalpha - 0.25 * math.pi)
            for c in PLANES:
                gj = ty * tile_rows + 3 * lanes_of((SB, LN)) + c - H
                gj = sel(gj < 0, -1 - gj, sel(gj >= cells, 2 * cells - 1 - gj, gj))
                tan_b = small_tan((gj.astype(F32) + 0.5) * dalpha - 0.25 * math.pi)[0:1, :]
                a_sq, b_sq = tan_a * tan_a, tan_b * tan_b
                r_sq = 1.0 + a_sq + b_sq
                sqrt_g = (1.0 + a_sq) * (1.0 + b_sq) / (r_sq * jnp.sqrt(r_sq))
                KK[0, c] = (0.5 * C_SPEED * CFL_STEP) / sqrt_g
                KK[1, c] = 1.0 - 4.0 * KK[0, c]

        @pl.loop(0, n_blocks)
        def _(b):
            fr = lax.rem(b, 2)

            for p in slots:
                pack_strips(QA, p, QA, p, 0, p)
            for p in slots:
                turn_strips(0, p, False)
            for p in slots:
                pack_corners(0, p)
            for p in slots:
                start_copies(0, fr, p)

            @pl.when(b == 0)
            def _():
                finish_winds()

            for p in slots:
                wait_copies(RECV, CRECV, recv_sem, crecv_sem, fr, p)
            for p in slots:
                unpack_cols(QA, p, fr, p)
            for p in slots:
                unpack_rows(QA, p, fr, p)
            for p in slots:
                wait_copies(SEND, CSEND, send_sem, csend_sem, 0, p)
            end = lax.div((b + 1) * steps, n_blocks)

            @pl.loop(lax.div(b * steps, n_blocks), end)
            def _(t):
                scale = ws_ref[t]
                stage(QA, QB, scale, False, True)
                stage(QB, QA, scale, True, t + 1 < end)

        store_field(QA)

    return kernel


def solution(mesh):
    tile_count = mesh.shape['tx']
    field_spec = P(('member', 'panel'), 'tx', 'ty')
    wind_spec = P('panel', 'tx', 'ty')

    def local_run(tracer, wind_a, wind_b, wind_scale):
        steps = wind_scale.shape[0]
        n_blocks = -(-steps // STEPS_PER_BLOCK)
        ext = SB * KR
        block = pl.BlockSpec((NPAN, ext, ext), lambda n: (0, 0, 0))
        dma = pltpu.SemaphoreType.DMA
        return pl.pallas_call(
            make_kernel(tile_count, steps, n_blocks, tracer.shape[1]),
            grid=(1,),
            out_shape=jax.ShapeDtypeStruct(tracer.shape, F32),
            in_specs=[pl.BlockSpec(memory_space=pltpu.SMEM), block, block, block],
            out_specs=block,
            scratch_shapes=[
                pltpu.VMEM((NPAN, NC, ext + 32, LN), F32),
                pltpu.VMEM((NPAN, NC, ext + 32, LN), F32),
                pltpu.VMEM((2 * NPAN, NC, ext + 32, LN), F32),
                pltpu.VMEM((NPAN, 2, NC, SB, LN), F32),
                pltpu.VMEM((2, NC, ext, LN), F32),
                pltpu.VMEM((NC, ext + 32, LN), F32),
                pltpu.VMEM((NC, ext + 32, LN), F32),
                pltpu.VMEM((9, LN, LN), F32),
                pltpu.VMEM((3, NPAN, 4, NC, H, LN), F32),
                pltpu.VMEM((4, NPAN, 4, NC, H, LN), F32),
                pltpu.VMEM((3, NPAN, 4, H, LN), F32),
                pltpu.VMEM((4, NPAN, 4, H, LN), F32),
                *[dma((n, NPAN, 4)) for n in (3, 4, 3, 4)],
            ],
            compiler_params=pltpu.CompilerParams(collective_id=0, has_side_effects=True, vmem_limit_bytes=60 * 1024 * 1024),
            cost_estimate=pl.CostEstimate(flops=10 ** 9, bytes_accessed=10 ** 7, transcendentals=0),
        )(wind_scale, tracer, wind_a, wind_b)

    return jax.shard_map(local_run, mesh=mesh, in_specs=(field_spec, wind_spec, wind_spec, P()),
                         out_specs=field_spec, check_vma=False)
```

time: 134 us -> 136 us (1.015)
    pallas_call x1, Pallas kernels: 132 us -> 133 us  [local_run(): pl.pallas_call(make_kernel(tile_count, steps, n_blocks, tracer.shape[1]),...]
where the time goes in v2:
time: 136 us
  Pallas kernels  133 us (98%)
  local copies, waits for them, and re-layouts  2.72 us (2%)
    pallas_call x1, Pallas kernels, local_run(): pl.pallas_call(make_kernel(tile_count, steps, n_blocks, tracer.shape[1]),...  133 us

profile of v2, /device:TPU:97, one launch (start us, length us, event | category | flops | bytes accessed | tf_op | source)
XLA Modules:
  0.0 135.9 jit_solution(17478627800921794002)
XLA Ops:
  0.0 133.2 %shard_map.46 = f32[3,360,360]{2,1,0:T(8,128)} custom-call(f32[16]{0:T(128)} %ws_ref.1, f32[3,360,360]{2,1,0:T(8,128)} %q_in.1, f32[3,360,360]{2,1,0:T(8,128)} %a_in.1, f32[3,360,360]{2,1,0:T(8,128)} %b_in.1), custom_call_target="tpu_custom_call" | custom-call | flops 1000000000 | bytes 10000000 | tf_op jit(solution)/shard_map/pallas_call | solution.py:556
  133.2 2.7 %copy.6 = f32[3,360,360]{2,1,0:T(8,128)} copy(f32[3,360,360]{2,1,0:T(8,128)} %shard_map.46) | data formatting | bytes 3110400

commit v3 on v2

--- a/solution.py
+++ b/solution.py
@@ -114,8 +114,18 @@
         corners = [(sa, sb) for sa in range(2) for sb in range(2)]
         slots = range(NPAN)
         strip_to = [[dest(p, side, 0)[:3] for side in SIDES] for p in slots]
-        stays = [[is_here(plan[0]) for plan in row] for row in strip_to]
+        stays = [[sel(is_here(plan[0]), 1, 0) for plan in row] for row in strip_to]
         corner_to = [[corner_plan(p, sa, sb) for sa, sb in corners] for p in slots]
+        flips = [[sel(at_edge(side), neighbour(p, side)[3], 0) for side in SIDES] for p in slots]
+        turns = [[sel(at_edge(side), neighbour(p, side)[4], 0) for side in SIDES] for p in slots]
+
+        def at_slot(p, table):
+            first = table[0]
+            if isinstance(first, dict):
+                return {key: at_slot(p, [row[key] for row in table]) for key in first}
+            if isinstance(first, (tuple, list)):
+                return [at_slot(p, [row[n] for row in table]) for n in range(len(first))]
+            return sel(p == 0, first, sel(p == 1, table[1], table[2]))
         mesh_ids = pl.DeviceIdType.MESH
 
         barrier = pltpu.get_barrier_semaphore()
@@ -189,37 +199,36 @@
                     SEND[f, p, 3, cp, quarter(c), :] = t[high:high + GL]
 
         def turn_strips(f, p, winds):
+            flip_at, turn_at = at_slot(p, flips), at_slot(p, turns)
             for side in SIDES:
-                _, _, _, flip, turned = neighbour(p, side)
-                if not isinstance(flip, int) or flip:
-                    @pl.when(sel(at_edge(side), flip, 0) == 1)
-                    def _():
-                        inside = lanes_of((NC * H, LN))
-                        inside = jnp.logical_and(inside >= GL, inside < LN - GL)
-                        old = jnp.concatenate([SEND[f, p, side, NC - 1 - c] for c in PLANES], axis=0)
-                        mirror = (rows_of((LN, LN)) + lanes_of((LN, LN)) == LN - 1).astype(F32)
-                        new = jnp.dot(sel(inside, old, 0.0), mirror, precision=lax.Precision.HIGHEST,
-                                      preferred_element_type=F32)
-                        for c in PLANES:
-                            SEND[f, p, side, c] = new[H * c:H * (c + 1)]
+                @pl.when(flip_at[side] == 1)
+                def _():
+                    inside = lanes_of((NC * H, LN))
+                    inside = jnp.logical_and(inside >= GL, inside < LN - GL)
+                    old = jnp.concatenate([SEND[f, p, side, NC - 1 - c] for c in PLANES], axis=0)
+                    mirror = (rows_of((LN, LN)) + lanes_of((LN, LN)) == LN - 1).astype(F32)
+                    new = jnp.dot(jnp.where(inside, old, 0.0), mirror, precision=lax.Precision.HIGHEST,
+                                  preferred_element_type=F32)
+                    for c in PLANES:
+                        SEND[f, p, side, c] = new[H * c:H * (c + 1)]
+                    if winds:
+                        @pl.when(f == 2)
+                        def _():
+                            for c in PLANES:
+                                SEND[f, p, side, c] = -SEND[f, p, side, c]
+
+                @pl.when(turn_at[side] == 1)
+                def _():
+                    for c in PLANES:
+                        v = SEND[f, p, side, c]
                         if winds:
-                            @pl.when(f == 2)
-                            def _():
-                                for c in PLANES:
-                                    SEND[f, p, side, c] = -SEND[f, p, side, c]
-                if not isinstance(turned, int) or turned:
-                    @pl.when(sel(at_edge(side), turned, 0) == 1)
-                    def _():
-                        for c in PLANES:
-                            v = SEND[f, p, side, c]
-                            if winds:
-                                v = sel(f == 1, -v, v)
-                            for m in range(H):
-                                SEND[f, p, side, c, m:m + 1, :] = v[H - 1 - m:H - m, :]
-
-        def pack_corners(f, p):
+                            v = sel(f == 1, -v, v)
+                        for m in range(H):
+                            SEND[f, p, side, c, m:m + 1, :] = v[H - 1 - m:H - m, :]
+
+        def pack_corners(f, p, plan):
             lane = lanes_of((H, LN))
-            for cid, (_, _, _, side, x) in enumerate(corner_to[p]):
+            for cid, (_, _, _, side, x) in enumerate(plan):
                 hi = lo = None
                 for c in PLANES:
                     v = SEND[f, p, side, c]
@@ -228,16 +237,20 @@
                     lo = vl if c == 0 else sel(lane < LN - GL * c, vl, lo)
                 CSEND[f, p, cid] = sel(x == 1, hi, lo)
 
-        def start_copies(f, fr, p):
+        def send_panel(row_ref, row_at, col_ref, col_at, f, fr, p, winds):
+            pack_strips(row_ref, row_at, col_ref, col_at, f, p)
+            turn_strips(f, p, winds)
+            plan = at_slot(p, corner_to)
+            pack_corners(f, p, plan)
+            to, here_at = at_slot(p, strip_to), at_slot(p, stays)
             for side in SIDES:
-                device, slot, dside = strip_to[p][side]
-                here = stays[p][side]
-
-                @pl.when(here)
+                device, slot, dside = to[side]
+
+                @pl.when(here_at[side] == 1)
                 def _():
                     RECV[fr, slot, dside] = SEND[f, p, side]
 
-                @pl.when(jnp.logical_not(here))
+                @pl.when(here_at[side] == 0)
                 def _():
                     pltpu.make_async_remote_copy(
                         src_ref=SEND.at[f, p, side], dst_ref=RECV.at[fr, slot, dside], send_sem=send_sem.at[f, p, side],
@@ -245,14 +258,14 @@
             for cid, (sa, sb) in enumerate(corners):
                 @pl.when(has_corner(sa, sb))
                 def _():
-                    device, slot, dcorner, _, _ = corner_to[p][cid]
+                    device, slot, dcorner, _, _ = plan[cid]
                     pltpu.make_async_remote_copy(
                         src_ref=CSEND.at[f, p, cid], dst_ref=CRECV.at[fr, slot, dcorner], send_sem=csend_sem.at[f, p, cid],
                         recv_sem=crecv_sem.at[fr, slot, dcorner], device_id=device, device_id_type=mesh_ids).start()
 
         def wait_copies(strips, blocks, sem, csem, f, p):
             for side in SIDES:
-                @pl.when(jnp.logical_not(stays[p][side]))
+                @pl.when(stays[p][side] == 0)
                 def _():
                     pltpu.make_async_copy(strips.at[f, p, side], strips.at[f, p, side], sem.at[f, p, side]).wait()
             for cid, (sa, sb) in enumerate(corners):
@@ -426,7 +439,7 @@
                 dst[p, :, pl.ds(SB * (k + 2), SB), :] = new
                 x_low, q_now, e_now, g_now, q_next = x_high, q_next, e_next, g_next, q_far
 
-        def stage(src, dst, scale, second, more):
+        def stage(src, dst, scale, second, more, after=None):
             pad_rows(src)
 
             @pl.when(more)
@@ -436,6 +449,8 @@
             @pl.loop(0, NPAN)
             def _(p):
                 panel_pass(src, dst, p, scale, second)
+                if after is not None:
+                    after(p)
 
         load_field(a_in, WW, WA)
         load_field(b_in, WW, WB)
@@ -446,13 +461,7 @@
         def _(f):
             @pl.loop(0, NPAN)
             def _(p):
-                pack_strips(WW, (f - 1) * NPAN + p, WW, (2 - f) * NPAN + p, f, p)
-            for p in slots:
-                turn_strips(f, p, True)
-            for p in slots:
-                pack_corners(f, p)
-            for p in slots:
-                start_copies(f, f + 1, p)
+                send_panel(WW, (f - 1) * NPAN + p, WW, (2 - f) * NPAN + p, f, f + 1, p, True)
         load_field(q_in, QA, 0)
 
         def finish_winds():
@@ -508,14 +517,11 @@
         def _(b):
             fr = lax.rem(b, 2)
 
-            for p in slots:
-                pack_strips(QA, p, QA, p, 0, p)
-            for p in slots:
-                turn_strips(0, p, False)
-            for p in slots:
-                pack_corners(0, p)
-            for p in slots:
-                start_copies(0, fr, p)
+            @pl.when(b == 0)
+            def _():
+                @pl.loop(0, NPAN)
+                def _(p):
+                    send_panel(QA, p, QA, p, 0, 0, p, False)
 
             @pl.when(b == 0)
             def _():
@@ -535,7 +541,12 @@
             def _(t):
                 scale = ws_ref[t]
                 stage(QA, QB, scale, False, True)
-                stage(QB, QA, scale, True, t + 1 < end)
+
+                def after(p):
+                    @pl.when(jnp.logical_and(t + 1 == end, b + 1 < n_blocks))
+                    def _():
+                        send_panel(QA, p, QA, p, 0, 1 - fr, p, False)
+                stage(QB, QA, scale, True, t + 1 < end, after)
 
         store_field(QA)
 

time: 136 us -> 136 us (level)
  no operation moved by 1% of the time
where the time goes in v3:
time: 136 us
  Pallas kernels  133 us (98%)
  local copies, waits for them, and re-layouts  2.72 us (2%)
    pallas_call x1, Pallas kernels, local_run(): pl.pallas_call(make_kernel(tile_count, steps, n_blocks, tracer.shape[1]),...  133 us

profile of v3, /device:TPU:97, one launch (start us, length us, event | category | flops | bytes accessed | tf_op | source)
XLA Modules:
  0.0 135.6 jit_solution(11142189419777420154)
XLA Ops:
  0.0 132.9 %shard_map.46 = f32[3,360,360]{2,1,0:T(8,128)} custom-call(f32[16]{0:T(128)} %ws_ref.1, f32[3,360,360]{2,1,0:T(8,128)} %q_in.1, f32[3,360,360]{2,1,0:T(8,128)} %a_in.1, f32[3,360,360]{2,1,0:T(8,128)} %b_in.1), custom_call_target="tpu_custom_call" | custom-call | flops 1000000000 | bytes 10000000 | tf_op jit(solution)/shard_map/pallas_call | solution.py:567
  132.9 2.7 %copy.6 = f32[3,360,360]{2,1,0:T(8,128)} copy(f32[3,360,360]{2,1,0:T(8,128)} %shard_map.46) | data formatting | bytes 3110400

commit v4 on v3

--- a/solution.py
+++ b/solution.py
@@ -20,6 +20,7 @@
 SB = 8
 LN = 128
 GL = 4
+BETA_SHIFT = 71
 STEPS_PER_BLOCK = 3
 BETA_ROWS = 4
 F32 = jnp.float32
@@ -99,11 +100,10 @@
                 device, slot, dside, flip = dest(p, side, off)
                 x = end + flip * (1 - 2 * end)
                 e = 1 - x
-                plans.append((device, slot, sel(dside < 2, 2 * dside + e, 2 * e + (dside - 2)), side, x))
-            (dv_a, sl_a, dc_a, s_a, x_a), (dv_b, sl_b, dc_b, s_b, x_b) = plans
-            device = {key: sel(out_b, dv_b[key], dv_a[key]) for key in dv_a}
-            return (device, sel(out_b, sl_b, sl_a), sel(out_b, dc_b, dc_a),
-                    sel(out_b, s_b, s_a), sel(out_b, x_b, x_a))
+                plans.append((device, slot, sel(dside < 2, 2 * dside + e, 2 * e + (dside - 2)), side, x,
+                              sel(dside < 2, 0, 1)))
+            device = {key: sel(out_b, plans[1][0][key], plans[0][0][key]) for key in plans[0][0]}
+            return (device, *[sel(out_b, second, first) for first, second in zip(plans[0][1:], plans[1][1:])])
 
         def has_corner(sa, sb):
             return jnp.logical_not(jnp.logical_and(at_edge(sa), at_edge(2 + sb)))
@@ -182,11 +182,11 @@
 
             def window(first):
                 return jnp.logical_and(lane >= first, lane < first + GL)
+            planes = [col_ref[col_at, c, pl.ds(2 * SB, SB * KR), :].reshape(2 * SB, NC * SB, LN) for c in PLANES]
             for cp in PLANES:
                 mix = None
                 for c in PLANES:
-                    blk = jnp.concatenate([col_ref[col_at, c, pl.ds(SB * (cp + 2) + s, 2 * SB, stride=NC * SB), :]
-                                           for s in range(SB)], axis=0)
+                    blk = planes[c][:, SB * cp:SB * (cp + 1)].reshape(LN, LN)
                     if c == 0:
                         mix = blk
                     else:
@@ -198,21 +198,37 @@
                     SEND[f, p, 2, cp, quarter(c), :] = t[low:low + GL]
                     SEND[f, p, 3, cp, quarter(c), :] = t[high:high + GL]
 
+        def beta_order(lane):
+            return 2 * SB * lax.rem(lane, SB) + lax.div(lane, SB)
+
+        def beta_lane(n):
+            return SB * lax.rem(n, 2 * SB) + lax.div(n, 2 * SB)
+
         def turn_strips(f, p, winds):
-            flip_at, turn_at = at_slot(p, flips), at_slot(p, turns)
+            flip_at, turn_at, to = at_slot(p, flips), at_slot(p, turns), at_slot(p, strip_to)
             for side in SIDES:
-                @pl.when(flip_at[side] == 1)
-                def _():
-                    inside = lanes_of((NC * H, LN))
-                    inside = jnp.logical_and(inside >= GL, inside < LN - GL)
-                    old = jnp.concatenate([SEND[f, p, side, NC - 1 - c] for c in PLANES], axis=0)
-                    mirror = (rows_of((LN, LN)) + lanes_of((LN, LN)) == LN - 1).astype(F32)
-                    new = jnp.dot(jnp.where(inside, old, 0.0), mirror, precision=lax.Precision.HIGHEST,
+                to_beta = to[side][2] >= 2
+                moved = jnp.logical_not(to_beta) if side >= 2 else to_beta
+
+                @pl.when(jnp.logical_or(flip_at[side] == 1, moved))
+                def _():
+                    back = flip_at[side] == 1
+                    at = lanes_of((NC * H, LN))
+                    at = beta_order(at) if side >= 2 else at
+                    inside = jnp.logical_and(at >= GL, at < LN - GL)
+                    now = [SEND[f, p, side, c] for c in PLANES]
+                    old = jnp.concatenate([sel(back, now[NC - 1 - c], now[c]) for c in PLANES], axis=0)
+                    come = lanes_of((LN, LN))
+                    come = sel(to_beta, beta_order(come), come)
+                    come = sel(back, LN - 1 - come, come)
+                    come = beta_lane(come) if side >= 2 else come
+                    place = (rows_of((LN, LN)) == come).astype(F32)
+                    new = jnp.dot(sel(inside, old, jnp.zeros_like(old)), place, precision=lax.Precision.HIGHEST,
                                   preferred_element_type=F32)
                     for c in PLANES:
                         SEND[f, p, side, c] = new[H * c:H * (c + 1)]
                     if winds:
-                        @pl.when(f == 2)
+                        @pl.when(jnp.logical_and(f == 2, back))
                         def _():
                             for c in PLANES:
                                 SEND[f, p, side, c] = -SEND[f, p, side, c]
@@ -228,14 +244,18 @@
 
         def pack_corners(f, p, plan):
             lane = lanes_of((H, LN))
-            for cid, (_, _, _, side, x) in enumerate(plan):
-                hi = lo = None
+            for cid, (_, _, _, side, x, to_beta) in enumerate(plan):
+                beta, high = to_beta == 1, x == 1
+                key = sel(beta, lax.rem(lane, SB), lane)
+                key = sel(high, key, sel(beta, SB - 1, LN - 1) - key)
+                step = sel(beta, 1, GL)
+                first = sel(beta, LN - BETA_SHIFT, SB)
+                msg = None
                 for c in PLANES:
-                    v = SEND[f, p, side, c]
-                    vh, vl = pltpu.roll(v, SB + GL * c, 1), pltpu.roll(v, LN - SB - GL * c, 1)
-                    hi = vh if c == 0 else sel(lane >= GL * c, vh, hi)
-                    lo = vl if c == 0 else sel(lane < LN - GL * c, vl, lo)
-                CSEND[f, p, cid] = sel(x == 1, hi, lo)
+                    shift = sel(high, first + step * c, LN - first - step * c)
+                    v = pltpu.roll(SEND[f, p, side, c], shift, 1)
+                    msg = v if c == 0 else sel(key >= step * c, v, msg)
+                CSEND[f, p, cid] = msg
 
         def send_panel(row_ref, row_at, col_ref, col_at, f, fr, p, winds):
             pack_strips(row_ref, row_at, col_ref, col_at, f, p)
@@ -258,7 +278,7 @@
             for cid, (sa, sb) in enumerate(corners):
                 @pl.when(has_corner(sa, sb))
                 def _():
-                    device, slot, dcorner, _, _ = plan[cid]
+                    device, slot, dcorner = plan[cid][:3]
                     pltpu.make_async_remote_copy(
                         src_ref=CSEND.at[f, p, cid], dst_ref=CRECV.at[fr, slot, dcorner], send_sem=csend_sem.at[f, p, cid],
                         recv_sem=crecv_sem.at[fr, slot, dcorner], device_id=device, device_id_type=mesh_ids).start()
@@ -284,15 +304,16 @@
             for e in range(2):
                 cid = 2 * side + e if side < 2 else 2 * e + side - 2
                 msg = CRECV[fr, p, cid]
+                step = c if side >= 2 else GL * c
                 if c:
-                    msg = pltpu.roll(msg, 4 * c if e else LN - 4 * c, 1)
-                inside = lane >= 124 if e else lane < 4
+                    msg = pltpu.roll(msg, step if e else LN - step, 1)
+                at = beta_order(lane) if side >= 2 else lane
+                inside = at >= LN - GL if e else at < GL
                 v = sel(jnp.logical_and(inside, end_valid(side, e)), msg, v)
             return v
 
         def unpack_cols(ref, dst, fr, p):
-            lane = lanes_of((2 * SB, LN))
-            ghost = jnp.logical_or(lane < GL, lane >= LN - GL)
+            parts = []
             for cp in PLANES:
                 low, high = merged(fr, p, 2, cp), merged(fr, p, 3, cp)
                 z = ZS.at[NC * p + cp]
@@ -300,11 +321,13 @@
                     z[pl.ds(SB * c, GL), :] = low[GL * c:GL * (c + 1)]
                     z[pl.ds((SB * c - GL) % LN, GL), :] = high[GL * c:GL * (c + 1)]
                 t = z[...].T
-                for c in PLANES:
-                    tc = pltpu.roll(t, LN - SB * c, 1) if c else t
-                    for s in range(SB):
-                        rows = pl.ds(SB * (cp + 2) + s, 2 * SB, stride=NC * SB)
-                        ref[dst, c, rows, :] = sel(ghost, tc[2 * SB * s:2 * SB * (s + 1)], ref[dst, c, rows, :])
+                parts.append([(pltpu.roll(t, LN - SB * c, 1) if c else t).reshape(2 * SB, SB, LN) for c in PLANES])
+            lane = lanes_of((SB * KR, LN))
+            ghost = jnp.logical_or(lane < GL, lane >= LN - GL)
+            rows = pl.ds(2 * SB, SB * KR)
+            for c in PLANES:
+                new = jnp.concatenate([part[c] for part in parts], axis=1).reshape(SB * KR, LN)
+                ref[dst, c, rows, :] = sel(ghost, new, ref[dst, c, rows, :])
 
         def unpack_rows(ref, dst, fr, p):
             lane = lanes_of((GL, LN))

time: 136 us -> 136 us (level)
  no operation moved by 1% of the time
where the time goes in v4:
time: 136 us
  Pallas kernels  134 us (99%)
  local copies, waits for them, and re-layouts  2.72 us (2%)
    pallas_call x1, Pallas kernels, local_run(): pl.pallas_call(make_kernel(tile_count, steps, n_blocks, tracer.shape[1]),...  134 us

profile of v4, /device:TPU:97, one launch (start us, length us, event | category | flops | bytes accessed | tf_op | source)
XLA Modules:
  0.0 136.4 jit_solution(17597172732101340370)
XLA Ops:
  0.0 133.7 %shard_map.46 = f32[3,360,360]{2,1,0:T(8,128)} custom-call(f32[16]{0:T(128)} %ws_ref.1, f32[3,360,360]{2,1,0:T(8,128)} %q_in.1, f32[3,360,360]{2,1,0:T(8,128)} %a_in.1, f32[3,360,360]{2,1,0:T(8,128)} %b_in.1), custom_call_target="tpu_custom_call" | custom-call | flops 1000000000 | bytes 10000000 | tf_op jit(solution)/shard_map/pallas_call | solution.py:590
  133.7 2.7 %copy.6 = f32[3,360,360]{2,1,0:T(8,128)} copy(f32[3,360,360]{2,1,0:T(8,128)} %shard_map.46) | data formatting | bytes 3110400

commit v5 on v4

--- a/solution.py
+++ b/solution.py
@@ -418,7 +418,7 @@
             x1 = WW[WB + p, 1, rows, :] * (g1 + g2)
             x2 = WW[WB + p, 2, rows, :] * (g2 + g0r)
             x2l = roll_up(x2)
-            return jnp.stack([x0 - x2l, x1 - x0, x2 - x1]), jnp.stack([e0, e1, e2])
+            return jnp.stack([scale * (x0 - x2l) - e0, scale * (x1 - x0) - e1, scale * (x2 - x1) - e2])
 
         def row_group(ref, p, k):
             return ref[p, :, pl.ds(SB * (k + 2), SB), :]
@@ -450,13 +450,13 @@
                 if k % BETA_ROWS == 0:
                     beta = beta_rows(src, p, k, scale)
                 at = SB * (k % BETA_ROWS)
-                tb, eb = (v[:, at:at + SB] for v in beta)
+                tb = beta[:, at:at + SB]
                 q_far = load(k + 2)
                 e_next = q_now + q_far
                 g_next = 8.0 * q_next - e_next
                 x_high = row_group(WW, WA + p, k) * (g_now + g_next)
-                u = scale * (x_high - x_low + tb) - (e_now + eb)
-                new = KK[1, :, pl.ds(SB * k, SB), :] * q_now - KK[0, :, pl.ds(SB * k, SB), :] * u
+                u = scale * (x_high - x_low) - e_now + tb + 4.0 * q_now
+                new = q_now - KK[:, pl.ds(SB * k, SB), :] * u
                 if second:
                     new = 0.5 * (row_group(dst, p, k) + new)
                 dst[p, :, pl.ds(SB * (k + 2), SB), :] = new
@@ -533,8 +533,7 @@
                 a_sq, b_sq = tan_a * tan_a, tan_b * tan_b
                 r_sq = 1.0 + a_sq + b_sq
                 sqrt_g = (1.0 + a_sq) * (1.0 + b_sq) / (r_sq * jnp.sqrt(r_sq))
-                KK[0, c] = (0.5 * C_SPEED * CFL_STEP) / sqrt_g
-                KK[1, c] = 1.0 - 4.0 * KK[0, c]
+                KK[c] = (0.5 * C_SPEED * CFL_STEP) / sqrt_g
 
         @pl.loop(0, n_blocks)
         def _(b):
@@ -598,7 +597,7 @@
                 pltpu.VMEM((NPAN, NC, ext + 32, LN), F32),
                 pltpu.VMEM((2 * NPAN, NC, ext + 32, LN), F32),
                 pltpu.VMEM((NPAN, 2, NC, SB, LN), F32),
-                pltpu.VMEM((2, NC, ext, LN), F32),
+                pltpu.VMEM((NC, ext, LN), F32),
                 pltpu.VMEM((NC, ext + 32, LN), F32),
                 pltpu.VMEM((NC, ext + 32, LN), F32),
                 pltpu.VMEM((9, LN, LN), F32),

time: 136 us -> 139 us (1.022)
  Pallas kernels: 134 us -> 136 us
    pallas_call x1, Pallas kernels: 134 us -> 136 us  [local_run(): pl.pallas_call(make_kernel(tile_count, steps, n_blocks, tracer.shape[1]),...]
where the time goes in v5:
time: 139 us
  Pallas kernels  136 us (98%)
  local copies, waits for them, and re-layouts  2.72 us (2%)
    pallas_call x1, Pallas kernels, local_run(): pl.pallas_call(make_kernel(tile_count, steps, n_blocks, tracer.shape[1]),...  136 us

profile of v5, /device:TPU:97, one launch (start us, length us, event | category | flops | bytes accessed | tf_op | source)
XLA Modules:
  0.0 139.1 jit_solution(3522414466727208508)
XLA Ops:
  0.0 136.3 %shard_map.46 = f32[3,360,360]{2,1,0:T(8,128)} custom-call(f32[16]{0:T(128)} %ws_ref.1, f32[3,360,360]{2,1,0:T(8,128)} %q_in.1, f32[3,360,360]{2,1,0:T(8,128)} %a_in.1, f32[3,360,360]{2,1,0:T(8,128)} %b_in.1), custom_call_target="tpu_custom_call" | custom-call | flops 1000000000 | bytes 10000000 | tf_op jit(solution)/shard_map/pallas_call | solution.py:589
  136.4 2.7 %copy.6 = f32[3,360,360]{2,1,0:T(8,128)} copy(f32[3,360,360]{2,1,0:T(8,128)} %shard_map.46) | data formatting | bytes 3110400

commit v6 on v4

--- a/solution.py
+++ b/solution.py
@@ -552,9 +552,7 @@
 
             for p in slots:
                 wait_copies(RECV, CRECV, recv_sem, crecv_sem, fr, p)
-            for p in slots:
                 unpack_cols(QA, p, fr, p)
-            for p in slots:
                 unpack_rows(QA, p, fr, p)
             for p in slots:
                 wait_copies(SEND, CSEND, send_sem, csend_sem, 0, p)

time: 136 us -> 133 us (0.978)
  Pallas kernels: 134 us -> 130 us
    pallas_call x1, Pallas kernels: 134 us -> 130 us  [local_run(): pl.pallas_call(make_kernel(tile_count, steps, n_blocks, tracer.shape[1]),...]
where the time goes in v6:
time: 133 us
  Pallas kernels  130 us (98%)
  local copies, waits for them, and re-layouts  2.72 us (2%)
    pallas_call x1, Pallas kernels, local_run(): pl.pallas_call(make_kernel(tile_count, steps, n_blocks, tracer.shape[1]),...  130 us
    unnamed x1, local copies, waits for them, and re-layouts  2.72 us

profile of v6, /device:TPU:97, one launch (start us, length us, event | category | flops | bytes accessed | tf_op | source)
XLA Modules:
  0.0 132.9 jit_solution(4825414228471739700)
XLA Ops:
  0.0 130.2 %shard_map.46 = f32[3,360,360]{2,1,0:T(8,128)} custom-call(f32[16]{0:T(128)} %ws_ref.1, f32[3,360,360]{2,1,0:T(8,128)} %q_in.1, f32[3,360,360]{2,1,0:T(8,128)} %a_in.1, f32[3,360,360]{2,1,0:T(8,128)} %b_in.1), custom_call_target="tpu_custom_call" | custom-call | flops 1000000000 | bytes 10000000 | tf_op jit(solution)/shard_map/pallas_call | solution.py:588
  130.2 2.7 %copy.6 = f32[3,360,360]{2,1,0:T(8,128)} copy(f32[3,360,360]{2,1,0:T(8,128)} %shard_map.46) | data formatting | bytes 3110400

commit v7 on v6

--- a/solution.py
+++ b/solution.py
@@ -138,20 +138,19 @@
                 def _():
                     pl.semaphore_signal(barrier, inc=1, device_id=plan[0], device_id_type=mesh_ids)
 
-        def load_field(in_ref, dst, base):
+        def load_fields(jobs):
             @pl.loop(0, NPAN)
             def _(p):
-                for it in PLANES:
-                    for jt in PLANES:
-                        TT[it, pl.ds(H + LN * jt, LN), :] = in_ref[p, pl.ds(LN * it, LN), pl.ds(LN * jt, LN)].T
+                for f, (in_ref, _, _) in enumerate(jobs):
+                    for it in PLANES:
+                        for jt in PLANES:
+                            TT[NC * f + it, pl.ds(H + LN * jt, LN), :] = in_ref[p, pl.ds(LN * it, LN), pl.ds(LN * jt, LN)].T
+                        for c in PLANES:
+                            NN[NC * f + c, pl.ds(H + LN * it, LN), :] = TT[NC * f + it, pl.ds(c, LN, stride=NC), :].T
+                for f, (_, dst, base) in enumerate(jobs):
                     for c in PLANES:
-                        NN[c, pl.ds(H + LN * it, LN), :] = TT[it, pl.ds(c, LN, stride=NC), :].T
-
-                @pl.loop(0, KR // SB)
-                def _(kb):
-                    for c in PLANES:
-                        for k in range(SB):
-                            dst[base + p, c, pl.ds(pl.multiple_of(64 * kb + SB * (k + 2), SB), SB), :] = NN[c, pl.ds(SB * kb + k, SB, stride=KR), :]
+                        for k in range(KR):
+                            dst[base + p, c, pl.ds(SB * (k + 2), SB), :] = NN[NC * f + c, pl.ds(k, SB, stride=KR), :]
 
         def store_field(src):
             @pl.loop(0, NPAN)
@@ -475,8 +474,7 @@
                 if after is not None:
                     after(p)
 
-        load_field(a_in, WW, WA)
-        load_field(b_in, WW, WB)
+        load_fields([(a_in, WW, WA), (b_in, WW, WB)])
         is_cc = jnp.logical_and(jnp.logical_or(at_edge(0), at_edge(1)), jnp.logical_or(at_edge(2), at_edge(3)))
         pl.semaphore_wait(barrier, SB * NPAN - NPAN * sel(is_cc, 1, 0))
 
@@ -485,7 +483,7 @@
             @pl.loop(0, NPAN)
             def _(p):
                 send_panel(WW, (f - 1) * NPAN + p, WW, (2 - f) * NPAN + p, f, f + 1, p, True)
-        load_field(q_in, QA, 0)
+        load_fields([(q_in, QA, 0)])
 
         def finish_winds():
             metric()
@@ -597,8 +595,8 @@
                 pltpu.VMEM((2 * NPAN, NC, ext + 32, LN), F32),
                 pltpu.VMEM((NPAN, 2, NC, SB, LN), F32),
                 pltpu.VMEM((2, NC, ext, LN), F32),
-                pltpu.VMEM((NC, ext + 32, LN), F32),
-                pltpu.VMEM((NC, ext + 32, LN), F32),
+                pltpu.VMEM((2 * NC, ext + 32, LN), F32),
+                pltpu.VMEM((2 * NC, ext + 32, LN), F32),
                 pltpu.VMEM((9, LN, LN), F32),
                 pltpu.VMEM((3, NPAN, 4, NC, H, LN), F32),
                 pltpu.VMEM((4, NPAN, 4, NC, H, LN), F32),

time: 133 us -> 132 us (level)
  no operation moved by 1% of the time
where the time goes in v7:
time: 132 us
  Pallas kernels  129 us (98%)
  local copies, waits for them, and re-layouts  2.72 us (2%)
    pallas_call x1, Pallas kernels, local_run(): pl.pallas_call(make_kernel(tile_count, steps, n_blocks, tracer.shape[1]),...  129 us
    unnamed x1, local copies, waits for them, and re-layouts  2.72 us

profile of v7, /device:TPU:97, one launch (start us, length us, event | category | flops | bytes accessed | tf_op | source)
XLA Modules:
  0.0 131.9 jit_solution(16212315400304324225)
XLA Ops:
  0.0 129.2 %shard_map.46 = f32[3,360,360]{2,1,0:T(8,128)} custom-call(f32[16]{0:T(128)} %ws_ref.1, f32[3,360,360]{2,1,0:T(8,128)} %q_in.1, f32[3,360,360]{2,1,0:T(8,128)} %a_in.1, f32[3,360,360]{2,1,0:T(8,128)} %b_in.1), custom_call_target="tpu_custom_call" | custom-call | flops 1000000000 | bytes 10000000 | tf_op jit(solution)/shard_map/pallas_call | solution.py:586
  129.2 2.7 %copy.6 = f32[3,360,360]{2,1,0:T(8,128)} copy(f32[3,360,360]{2,1,0:T(8,128)} %shard_map.46) | data formatting | bytes 3110400

commit v8 on v7

--- a/solution.py
+++ b/solution.py
@@ -155,11 +155,9 @@
         def store_field(src):
             @pl.loop(0, NPAN)
             def _(p):
-                @pl.loop(0, KR // SB)
-                def _(kb):
-                    for c in PLANES:
-                        for k in range(SB):
-                            NN[c, pl.ds(SB * kb + k, SB, stride=KR), :] = src[p, c, pl.ds(pl.multiple_of(64 * kb + SB * (k + 2), SB), SB), :]
+                for c in PLANES:
+                    for k in range(KR):
+                        NN[c, pl.ds(k, SB, stride=KR), :] = src[p, c, pl.ds(SB * (k + 2), SB), :]
                 for it in PLANES:
                     for c in PLANES:
                         TT[it, pl.ds(c, LN, stride=NC), :] = NN[c, pl.ds(H + LN * it, LN), :].T
@@ -492,9 +490,6 @@
             def _(f):
                 for p in slots:
                     wait_copies(RECV, CRECV, recv_sem, crecv_sem, f + 1, p)
-
-                @pl.loop(0, NPAN)
-                def _(p):
                     unpack_cols(WW, (2 - f) * NPAN + p, f + 1, p)
 
             @pl.loop(1, 3)

time: 132 us -> 132 us (level)
  no operation moved by 1% of the time
where the time goes in v8:
time: 132 us
  Pallas kernels  129 us (98%)
  local copies, waits for them, and re-layouts  2.72 us (2%)
    pallas_call x1, Pallas kernels, local_run(): pl.pallas_call(make_kernel(tile_count, steps, n_blocks, tracer.shape[1]),...  129 us
    unnamed x1, local copies, waits for them, and re-layouts  2.72 us

profile of v8, /device:TPU:97, one launch (start us, length us, event | category | flops | bytes accessed | tf_op | source)
XLA Modules:
  0.0 131.9 jit_solution(11362554631155788748)
XLA Ops:
  0.0 129.2 %shard_map.46 = f32[3,360,360]{2,1,0:T(8,128)} custom-call(f32[16]{0:T(128)} %ws_ref.1, f32[3,360,360]{2,1,0:T(8,128)} %q_in.1, f32[3,360,360]{2,1,0:T(8,128)} %a_in.1, f32[3,360,360]{2,1,0:T(8,128)} %b_in.1), custom_call_target="tpu_custom_call" | custom-call | flops 1000000000 | bytes 10000000 | tf_op jit(solution)/shard_map/pallas_call | solution.py:581
  129.2 2.7 %copy.6 = f32[3,360,360]{2,1,0:T(8,128)} copy(f32[3,360,360]{2,1,0:T(8,128)} %shard_map.46) | data formatting | bytes 3110400

commit v9 on v7

--- a/solution.py
+++ b/solution.py
@@ -259,8 +259,6 @@
         def send_panel(row_ref, row_at, col_ref, col_at, f, fr, p, winds):
             pack_strips(row_ref, row_at, col_ref, col_at, f, p)
             turn_strips(f, p, winds)
-            plan = at_slot(p, corner_to)
-            pack_corners(f, p, plan)
             to, here_at = at_slot(p, strip_to), at_slot(p, stays)
             for side in SIDES:
                 device, slot, dside = to[side]
@@ -274,6 +272,8 @@
                     pltpu.make_async_remote_copy(
                         src_ref=SEND.at[f, p, side], dst_ref=RECV.at[fr, slot, dside], send_sem=send_sem.at[f, p, side],
                         recv_sem=recv_sem.at[fr, slot, dside], device_id=device, device_id_type=mesh_ids).start()
+            plan = at_slot(p, corner_to)
+            pack_corners(f, p, plan)
             for cid, (sa, sb) in enumerate(corners):
                 @pl.when(has_corner(sa, sb))
                 def _():

time: 132 us -> 131 us (level)
  no operation moved by 1% of the time
where the time goes in v9:
time: 131 us
  Pallas kernels  128 us (98%)
  local copies, waits for them, and re-layouts  2.72 us (2%)
    pallas_call x1, Pallas kernels, local_run(): pl.pallas_call(make_kernel(tile_count, steps, n_blocks, tracer.shape[1]),...  128 us
    unnamed x1, local copies, waits for them, and re-layouts  2.72 us

profile of v9, /device:TPU:97, one launch (start us, length us, event | category | flops | bytes accessed | tf_op | source)
XLA Modules:
  0.0 131.0 jit_solution(878326476726207880)
XLA Ops:
  0.0 128.3 %shard_map.46 = f32[3,360,360]{2,1,0:T(8,128)} custom-call(f32[16]{0:T(128)} %ws_ref.1, f32[3,360,360]{2,1,0:T(8,128)} %q_in.1, f32[3,360,360]{2,1,0:T(8,128)} %a_in.1, f32[3,360,360]{2,1,0:T(8,128)} %b_in.1), custom_call_target="tpu_custom_call" | custom-call | flops 1000000000 | bytes 10000000 | tf_op jit(solution)/shard_map/pallas_call | solution.py:586
  128.3 2.7 %copy.6 = f32[3,360,360]{2,1,0:T(8,128)} copy(f32[3,360,360]{2,1,0:T(8,128)} %shard_map.46) | data formatting | bytes 3110400
